TPU v7x, 32 devices: a whole 2x2x4 slice. The times are simulated.
32 devices in a mesh: seq: 4 (over z), tp: 8 (over y, x, core).
Axes of the slice: x: 2, y: 2, z: 4, core: 2. Of those that a mesh axis runs over, the one named last changes fastest.
Arguments:
- stream: float32 [512, 4, 2048], P(('seq', 'tp')), may hold values from -60 to 60
- norm_gain: float32 [2048], replicated, may hold values from 0.5 to 1.5
- norm_offset: float32 [2048], replicated, may hold values from -3 to 3
- attend_weight: bfloat16 [2048, 3, 2048], P(None, None, 'tp'), as said below
- attend_bias: float32 [3, 2048], P(None, 'tp'), may hold values from -3 to 3
- output_weight: bfloat16 [2048, 2048], P('tp'), may hold values from -2 to 2
- up_weight: bfloat16 [2048, 8192], P(None, 'tp'), may hold values from -0.125 to 0.125
- up_bias: float32 [8192], P('tp'), may hold values from -3 to 3
- down_weight: bfloat16 [8192, 2048], P('tp'), may hold values from -0.0625 to 0.0625
- final_bias: float32 [2048], replicated, may hold values from -3 to 3
- cotangent: float32 [512, 4, 2048], P(('seq', 'tp')), may hold values from -18 to 18
Outputs:
- result: float32 [512, 4, 2048], P(('seq', 'tp'))
- stream_grad: float32 [512, 4, 2048], P(('seq', 'tp'))
- norm_gain_grad: float32 [2048], replicated
- norm_offset_grad: float32 [2048], replicated
- attend_weight_grad: float32 [2048, 3, 2048], P(None, None, 'tp')
- attend_bias_grad: float32 [3, 2048], P(None, 'tp')
- output_weight_grad: float32 [2048, 2048], P('tp')
- up_weight_grad: float32 [2048, 8192], P(None, 'tp')
- up_bias_grad: float32 [8192], P('tp')
- down_weight_grad: float32 [8192, 2048], P('tp')
- final_bias_grad: float32 [2048], replicated
Inputs may be any that keep to these rules, and one draw needn't show every extreme that they name: `attend_weight`: entries of order one over the root of 2048.
All inputs are finite; a program needn't handle non-finite values.
Results may differ from a plain program's by a relative error of at most 0.012.
The roundings to bfloat16 on the way count: a program that leaves them out, or rounds other values in their place, can miss the bound.
Values may be sent and summed in bfloat16 or wider, within the bound.
A program may use at most 192 MiB of HBM per device.

v0:
```python
import math

import jax
import jax.numpy as jnp
from jax import lax
from jax.sharding import PartitionSpec as P

HEAD_DIM = 64
ROT = 32


EPS = 1e-05
GELU_C = 0.7978845608028654
CUBIC = 0.044715
LOG_BASE = math.log(10000.0)


def from_behind(value, axis, steps):
    count = lax.axis_size(axis)
    leading, last = (max(0, -steps), min(count, count - steps))
    return lax.ppermute(value, axis, [(source, source + steps) for source in range(leading, last)])


def from_behind_2(value, axis, by):
    devices = lax.axis_size(axis)
    return lax.ppermute(value, axis, [(i, (i + by) % devices) for i in range(devices)])


def gelu_parts(pre_act):
    inner_arg = GELU_C * (pre_act + CUBIC * pre_act * pre_act * pre_act)
    tanh_value = jnp.tanh(inner_arg)
    gelu_value = 0.5 * pre_act * (1.0 + tanh_value)
    gelu_slope = 0.5 * (1.0 + tanh_value) + 0.5 * pre_act * (
        1.0 - tanh_value * tanh_value
    ) * GELU_C * (1.0 + 3.0 * CUBIC * pre_act * pre_act)
    return (gelu_value, gelu_slope)


def rotary_angles(positions):
    half_rot = ROT // 2
    frequency = jnp.exp(jnp.arange(half_rot, dtype=jnp.float32) * (-2.0 * LOG_BASE / ROT))
    angles = positions.astype(jnp.float32)[:, None] * frequency[None, :]
    return (jnp.cos(angles), jnp.sin(angles))


def rotate(vectors, cosine, sine_table):
    half_rot = ROT // 2
    first_half = vectors[..., :half_rot]
    second_half = vectors[..., half_rot:ROT]
    return jnp.concatenate(
        [
            first_half * cosine - second_half * sine_table,
            second_half * cosine + first_half * sine_table,
            vectors[..., ROT:],
        ],
        axis=-1,
    )


def unrotate(vectors, cosine, sine_table):
    half_rot = ROT // 2
    first_half = vectors[..., :half_rot]
    second_half = vectors[..., half_rot:ROT]
    return jnp.concatenate(
        [
            first_half * cosine + second_half * sine_table,
            second_half * cosine - first_half * sine_table,
            vectors[..., ROT:],
        ],
        axis=-1,
    )


def transposed_dot(left_side, right_side):
    return lax.dot_general(
        left_side, right_side, (((1,), (1,)), ((), ())), preferred_element_type=jnp.float32
    )


def column_dot(left_side, right_side):
    return lax.dot_general(
        left_side, right_side, (((0,), (0,)), ((), ())), preferred_element_type=jnp.float32
    )


def pair_scores(queries, key_block, query_start, key_start, score_scale):
    scores = (
        jnp.einsum("qshd,kshd->shqk", queries, key_block, preferred_element_type=jnp.float32)
        * score_scale
    )
    query_place = query_start + jnp.arange(queries.shape[0], dtype=jnp.int32)
    key_place = key_start + jnp.arange(key_block.shape[0], dtype=jnp.int32)
    allowed = query_place[:, None] >= key_place[None, :]
    return jnp.where(allowed, scores, -jnp.inf)


def pair_grads(
    queries,
    context_grad,
    log_total,
    row_delta,
    key_block,
    value_block,
    query_start,
    key_start,
    score_scale,
):
    scores = pair_scores(queries, key_block, query_start, key_start, score_scale)
    probs = jnp.exp(scores - log_total[..., None])
    value_grad = jnp.einsum(
        "shqk,qshd->kshd",
        probs.astype(jnp.bfloat16),
        context_grad,
        preferred_element_type=jnp.float32,
    )
    prob_grad = jnp.einsum(
        "qshd,kshd->shqk", context_grad, value_block, preferred_element_type=jnp.float32
    )
    score_grad = (probs * (prob_grad - row_delta[..., None]) * score_scale).astype(jnp.bfloat16)
    query_grad = jnp.einsum(
        "shqk,kshd->qshd", score_grad, key_block, preferred_element_type=jnp.float32
    )
    key_grad = jnp.einsum(
        "shqk,qshd->kshd", score_grad, queries, preferred_element_type=jnp.float32
    )
    return (query_grad, key_grad, value_grad)


def cycle_pass(fold, state, key_value, cycle_index, cycle_size):
    state = fold(state, key_value, cycle_index)

    def forward_turn(turn_index, loop_state):
        kv_block, inner_state = loop_state
        kv_block = from_behind(kv_block, "seq", 1)
        return (kv_block, fold(inner_state, kv_block, (cycle_index - turn_index) % cycle_size))

    return lax.fori_loop(1, cycle_size, forward_turn, (key_value, state))[1]


def per_device(
    stream,
    norm_gain,
    norm_offset,
    attend_weight,
    attend_bias,
    output_weight,
    up_weight,
    up_bias,
    down_weight,
    final_bias,
    cotangent,
):
    piece_rows, seq_count, model_width = stream.shape
    local_width = attend_weight.shape[2]
    head_count = local_width // HEAD_DIM
    hidden_width = up_weight.shape[1]
    cycle_size = lax.axis_size("seq")
    block_len = piece_rows * lax.axis_size("tp")
    cycle_index = lax.axis_index("seq")
    block_start = cycle_index * block_len
    token_count = block_len * seq_count
    score_scale = HEAD_DIM ** (-0.5)
    head_shape = (block_len, seq_count, head_count, HEAD_DIM)
    row_mean = jnp.mean(stream, axis=-1, keepdims=True)
    centred = stream - row_mean
    inverse_std = lax.rsqrt(jnp.mean(centred * centred, axis=-1, keepdims=True) + EPS)
    unit_rows = centred * inverse_std
    normed = (unit_rows * norm_gain + norm_offset).astype(jnp.bfloat16)
    gathered = lax.all_gather(normed, "tp", axis=0, tiled=True)
    flat_normed = gathered.reshape(token_count, model_width)
    flat_attend = attend_weight.reshape(model_width, 3 * local_width)
    projected = jnp.dot(flat_normed, flat_attend, preferred_element_type=jnp.float32)
    projected = projected.reshape(
        block_len, seq_count, 3, head_count, HEAD_DIM
    ) + attend_bias.reshape(3, head_count, HEAD_DIM)
    cosine, sine_table = rotary_angles(block_start + jnp.arange(block_len, dtype=jnp.int32))
    cosine = cosine[:, None, None, :]
    sine_table = sine_table[:, None, None, :]
    queries = rotate(projected[:, :, 0], cosine, sine_table).astype(jnp.bfloat16)
    keys_own = rotate(projected[:, :, 1], cosine, sine_table).astype(jnp.bfloat16)
    values_own = projected[:, :, 2].astype(jnp.bfloat16)
    key_value = jnp.stack([keys_own, values_own]).reshape(2, block_len, seq_count, local_width)

    def absorb_stats(stat_state, kv_block, source):
        row_max, row_total = stat_state
        key_block = kv_block[0].reshape(head_shape)
        scores = pair_scores(queries, key_block, block_start, source * block_len, score_scale)
        new_max = jnp.maximum(row_max, jnp.max(scores, axis=-1))
        shrink = jnp.exp(row_max - new_max)
        row_total = row_total * shrink + jnp.sum(jnp.exp(scores - new_max[..., None]), axis=-1)
        return (new_max, row_total)

    start_stats = (
        jnp.full((seq_count, head_count, block_len), -jnp.inf, jnp.float32),
        jnp.zeros((seq_count, head_count, block_len), jnp.float32),
    )
    row_max, row_total = cycle_pass(absorb_stats, start_stats, key_value, cycle_index, cycle_size)
    log_total = row_max + jnp.log(row_total)

    def absorb_context(ctx_sum, kv_block, source):
        key_block = kv_block[0].reshape(head_shape)
        value_block = kv_block[1].reshape(head_shape)
        scores = pair_scores(queries, key_block, block_start, source * block_len, score_scale)
        weights = jnp.exp(scores - log_total[..., None]).astype(jnp.bfloat16)
        return ctx_sum + jnp.einsum(
            "shqk,kshd->shqd", weights, value_block, preferred_element_type=jnp.float32
        )

    ctx_sum = cycle_pass(
        absorb_context,
        jnp.zeros((seq_count, head_count, block_len, HEAD_DIM), jnp.float32),
        key_value,
        cycle_index,
        cycle_size,
    )
    context = jnp.transpose(ctx_sum.astype(jnp.bfloat16), (2, 0, 1, 3))
    context_rows = context.reshape(block_len, seq_count, local_width)
    up_pre = jnp.dot(flat_normed, up_weight, preferred_element_type=jnp.float32) + up_bias
    up_value, up_slope = gelu_parts(up_pre)
    up_hidden = up_value.astype(jnp.bfloat16).reshape(block_len, seq_count, hidden_width)
    row_count = lax.axis_size("tp") * piece_rows
    context_part = context_rows.reshape(row_count * seq_count, local_width)
    hidden_part = up_hidden.reshape(row_count * seq_count, hidden_width)
    summed = jnp.dot(context_part, output_weight, preferred_element_type=jnp.float32) + jnp.dot(
        hidden_part, down_weight, preferred_element_type=jnp.float32
    )
    branch_total = lax.psum_scatter(
        summed.reshape(row_count, seq_count, model_width), "tp", scatter_dimension=0, tiled=True
    )
    result = stream + branch_total + final_bias
    grad_rows = lax.all_gather(cotangent.astype(jnp.bfloat16), "tp", axis=0, tiled=True)
    grad_flat = grad_rows.reshape(token_count, model_width)
    context_flat = context_rows.reshape(token_count, local_width)
    hidden_flat = up_hidden.reshape(token_count, hidden_width)
    output_grad = column_dot(context_flat, grad_flat)
    down_grad = column_dot(hidden_flat, grad_flat)
    context_grad = transposed_dot(grad_flat, output_weight).astype(jnp.bfloat16).reshape(head_shape)
    pre_grad = transposed_dot(grad_flat, down_weight) * up_slope
    up_bias_grad = jnp.sum(pre_grad, axis=0)
    pre_rounded = pre_grad.astype(jnp.bfloat16)
    up_grad = column_dot(flat_normed, pre_rounded)
    row_delta = jnp.sum(context_grad.astype(jnp.float32) * context.astype(jnp.float32), axis=-1)
    row_delta = jnp.transpose(row_delta, (1, 2, 0))

    def key_turn(turn_index, kv_block, kv_acc, query_acc):
        source = (cycle_index - turn_index) % cycle_size
        query_part, key_part, value_part = pair_grads(
            queries,
            context_grad,
            log_total,
            row_delta,
            kv_block[0].reshape(head_shape),
            kv_block[1].reshape(head_shape),
            block_start,
            source * block_len,
            score_scale,
        )
        kv_acc = from_behind_2(
            kv_acc
            + jnp.stack([key_part, value_part]).reshape(2, block_len, seq_count, local_width),
            "seq",
            1,
        )
        return (kv_acc, query_acc + query_part)

    kv_acc = jnp.zeros((2, block_len, seq_count, local_width), jnp.float32)
    query_acc = jnp.zeros(head_shape, jnp.float32)
    kv_acc, query_acc = key_turn(0, key_value, kv_acc, query_acc)

    def key_loop(turn_index, loop_state):
        kv_block, kv_acc, query_acc = loop_state
        kv_block = from_behind(kv_block, "seq", 1)
        kv_acc, query_acc = key_turn(turn_index, kv_block, kv_acc, query_acc)
        return (kv_block, kv_acc, query_acc)

    loop_state = lax.fori_loop(1, cycle_size, key_loop, (key_value, kv_acc, query_acc))
    query_grad = loop_state[2]
    key_grad = loop_state[1][0].reshape(head_shape)
    value_grad = loop_state[1][1].reshape(head_shape)
    query_pre = unrotate(query_grad, cosine, sine_table)
    key_pre = unrotate(key_grad, cosine, sine_table)
    proj_grad = jnp.stack([query_pre, key_pre, value_grad], axis=2)
    attend_bias_grad = jnp.sum(proj_grad, axis=(0, 1)).reshape(3, local_width)
    proj_rows = proj_grad.astype(jnp.bfloat16).reshape(block_len, seq_count, 3 * local_width)
    attend_grad = column_dot(flat_normed, proj_rows.reshape(token_count, 3 * local_width)).reshape(
        model_width, 3, local_width
    )
    pre_rows = pre_rounded.reshape(block_len, seq_count, hidden_width)
    row_count = lax.axis_size("tp") * piece_rows
    proj_part = proj_rows.reshape(row_count * seq_count, 3 * local_width)
    pre_part = pre_rows.reshape(row_count * seq_count, hidden_width)
    summed = transposed_dot(proj_part, flat_attend) + transposed_dot(pre_part, up_weight)
    normed_grad = lax.psum_scatter(
        summed.reshape(row_count, seq_count, model_width), "tp", scatter_dimension=0, tiled=True
    )
    gain_part = jnp.sum(normed_grad * unit_rows, axis=(0, 1))
    offset_part = jnp.sum(normed_grad, axis=(0, 1))
    final_part = jnp.sum(cotangent, axis=(0, 1))
    scaled = normed_grad * norm_gain
    stream_grad = cotangent + inverse_std * (
        scaled
        - jnp.mean(scaled, axis=-1, keepdims=True)
        - unit_rows * jnp.mean(scaled * unit_rows, axis=-1, keepdims=True)
    )
    norm_sums = lax.psum((gain_part, offset_part, final_part), ("seq", "tp"))
    weight_sums = lax.psum(
        (attend_grad, attend_bias_grad, output_grad, up_grad, up_bias_grad, down_grad), "seq"
    )
    return (
        result,
        stream_grad,
        norm_sums[0],
        norm_sums[1],
        weight_sums[0],
        weight_sums[1],
        weight_sums[2],
        weight_sums[3],
        weight_sums[4],
        weight_sums[5],
        norm_sums[2],
    )


def solution(mesh):
    in_specs = (
        P(("seq", "tp"), None, None),
        P(),
        P(),
        P(None, None, "tp"),
        P(None, "tp"),
        P("tp", None),
        P(None, "tp"),
        P("tp"),
        P("tp", None),
        P(),
        P(("seq", "tp"), None, None),
    )
    out_specs = (
        P(("seq", "tp"), None, None),
        P(("seq", "tp"), None, None),
        P(),
        P(),
        P(None, None, "tp"),
        P(None, "tp"),
        P("tp", None),
        P(None, "tp"),
        P("tp"),
        P("tp", None),
        P(),
    )
    return jax.shard_map(
        per_device, mesh=mesh, in_specs=in_specs, out_specs=out_specs, check_vma=False
    )
```

profile of v0, /device:TPU:0, one launch (start us, length us, event | category | flops | bytes accessed | tf_op | source)
XLA Modules:
  0.0 1268.7 jit_solution(5240893005426542675)
XLA Ops:
  19.9 23.5 %all-gather.3.cloned.1.call-done = bf16[128,4,2048]{2,0,1:T(8,128)(2,1)} async-done(((bf16[16,4,2048]{2,0,1:T(8,128)(2,1)}), bf16[128,4,2048]{2,0,1:T(8,128)(2,1)}) %all-gather.3.cloned.1.call-update) | async-done | bytes 2097168 | tf_op jit(solution)/shard_map/all_gather | solution.py:169
  77.3 8.6 fusion.71
  88.0 49.2 %while.55 = (s32[]{:T(128)}, bf16[2,128,4,256]{1,3,2,0:T(8,128)(2,1)}, f32[4,4,128]{2,1,0:T(4,128)S(1)}, f32[4,4,128]{2,1,0:T(4,128)S(1)}, s32[]{:T(128)}, /*ind...) while((s32[]{:T(128)}, ...), condition=%wide.region_7.8_spmd, body=%wide.region_4.7_spmd.sunk | while | flops 34885904 | bytes 6433066 | solution.py:137
  91.6 11.7 collective-permute-done
  109.2 10.9 collective-permute-done
  125.9 10.0 collective-permute-done
  140.0 51.0 %while.56 = (s32[]{:T(128)}, bf16[2,128,4,256]{1,3,2,0:T(8,128)(2,1)}, f32[4,4,128,64]{2,3,1,0:T(8,128)}, s32[]{:T(128)}, s32[]{:T(128)}, /*index=5*/bf16[128,4,...) while((s32[]{:T(128)}, ...), condition=%wide.region_9.10_spmd, body=%wide.region_8.9_spmd.sunk | while | flops 68305168 | bytes 6072618 | solution.py:137
  144.5 9.2 collective-permute-done.1
  162.3 8.3 collective-permute-done.1
  179.4 7.4 collective-permute-done.1
  213.7 6.9 fusion.47
  222.8 108.4 %while.57 = (s32[]{:T(128)}, bf16[2,128,4,256]{1,3,2,0:T(8,128)(2,1)S(1)}, f32[2,128,4,256]{1,3,2,0:T(8,128)S(1)}, f32[128,4,4,64]{0,3,2,1:T(8,128)S(1)}, s32[]{...) while((s32[]{:T(128)}, ...), condition=%wide.region_13.14_spmd, body=%wide.region_12.13_spmd.sunk | while | flops 170541328 | bytes 20236648 | solution.py:276
  226.1 7.9 collective-permute-done.2
  239.5 18.3 %collective-permute-done.3 = f32[2,128,4,256]{1,3,2,0:T(8,128)S(1)} collective-permute-done((f32[2,128,4,256]{1,3,2,0:T(8,128)S(1)}, f32[2,128,4,256]{1,3,2,0:T(8,128)S(1)}, u32[]{:S(2)}, u32[]{:S(2)}) %collective-permute-start.3) | collective-permute-done | bytes 1048608 | tf_op jit(solution)/shard_map/while/body/eval_jaxpr/ppermute | solution.py:26
  262.4 9.4 collective-permute-done.2
  277.3 18.3 %collective-permute-done.3 = f32[2,128,4,256]{1,3,2,0:T(8,128)S(1)} collective-permute-done((f32[2,128,4,256]{1,3,2,0:T(8,128)S(1)}, f32[2,128,4,256]{1,3,2,0:T(8,128)S(1)}, u32[]{:S(2)}, u32[]{:S(2)}) %collective-permute-start.3) | collective-permute-done | bytes 1048608 | tf_op jit(solution)/shard_map/while/body/eval_jaxpr/ppermute | solution.py:26
  300.2 11.3 collective-permute-done.2
  317.1 14.1 %collective-permute-done.3 = f32[2,128,4,256]{1,3,2,0:T(8,128)S(1)} collective-permute-done((f32[2,128,4,256]{1,3,2,0:T(8,128)S(1)}, f32[2,128,4,256]{1,3,2,0:T(8,128)S(1)}, u32[]{:S(2)}, u32[]{:S(2)}) %collective-permute-start.3) | collective-permute-done | bytes 1048608 | tf_op jit(solution)/shard_map/while/body/eval_jaxpr/ppermute | solution.py:26
  337.1 7.0 convolution_add_fusion.1
  349.2 6.6 copy.128
  381.0 11.4 all-reduce.2
  394.4 11.9 reduce-scatter.2.cloned.1.call-done
  410.6 45.8 %all-reduce.1 = (f32[2048]{0:T(1024)}, f32[2048]{0:T(1024)}, f32[2048]{0:T(1024)}) all-reduce(f32[2048]{0:T(1024)S(1)} %get-tuple-element.734, f32[2048]{0:T(1024)S(1)} %get-tuple-element.737, f32[2048]{0:T(1024)S(1)} %copy-done.37), channel_id=1, replica_groups=mesh['seq'=4,'tp'=8] {'seq','tp'}, use_global_device_ids=true, to_apply=%region_18.19 | all-reduce | flops 6144 | bytes 49152 | tf_op jit(solution)/shard_map/psum | solution.py:305
  456.4 787.5 %all-reduce.9.cloned.1.call-done = (f32[2048,3,256]{2,0,1:T(8,128)}, f32[256,2048]{1,0:T(8,128)}, f32[2048,1024]{1,0:T(8,128)}, f32[1024,2048]{1,0:T(8,128)}) async-done(((f32[2048,3,256]{2,0,1:T(8,128)}, f32[256,2048]{1,0:T(8,128)}, f32[2048,1024]{1,0:T(8,128)}, f32[1024,2048]{1,0:T(8,128)}), (f32[2048,3,256]{2,0,1:T(8,128)}, f32[256,2048]{1,0:T(8,128)}, f32[2048,1024]{1,0:T(8,128)}, ...) | async-done | bytes 25165840 | tf_op jit(solution)/shard_map/psum | solution.py:306
  (280 shorter events, 206.4 us)
Async XLA Ops:
  7.2 78.7 %copy-start = (bf16[256,2048]{1,0:T(8,128)(2,1)S(1)}, bf16[256,2048]{1,0:T(8,128)(2,1)}, u32[]{:S(2)}) copy-start(bf16[256,2048]{1,0:T(8,128)(2,1)} %param.22) | copy-start | bytes 3145732
  7.2 36.2 %all-gather.3.cloned.1.call-start = ((), (), s32[]{:S(2)}) async-start(), calls=%async_computation.1 | async-start | bytes 2359296 | tf_op jit(solution)/shard_map/all_gather | solution.py:169
  12.8 60.4 %all-gather.5.cloned.1.call-start = ((), (), s32[]{:S(2)}) async-start(), calls=%async_computation.2 | async-start | bytes 2359296 | tf_op jit(solution)/shard_map/all_gather | solution.py:231
  14.3 378.1 %all-reduce.7.cloned.1.call-start = ((), (), s32[]{:S(2)}) async-start(), calls=%async_computation.4 | async-start | bytes 8388608
  48.0 39.4 %copy-start.27 = (bf16[128,4,4,32]{0,3,2,1:T(8,128)(2,1)}, bf16[128,4,4,32]{0,3,2,1:T(8,128)(2,1)S(1)}, u32[]{:S(2)}) copy-start(bf16[128,4,4,32]{0,3,2,1:T(8,128)(2,1)S(1)} %slice.166) | copy-start | bytes 393220
  49.0 38.4 %copy-start.19 = (bf16[128,4,4,16]{0,3,2,1:T(8,128)(2,1)}, bf16[128,4,4,16]{0,3,2,1:T(8,128)(2,1)S(1)}, u32[]{:S(2)}) copy-start(bf16[128,4,4,16]{0,3,2,1:T(8,128)(2,1)S(1)} %get-tuple-element.825) | copy-start | bytes 196612
  49.0 38.4 %copy-start.21 = (bf16[128,4,4,16]{0,3,2,1:T(8,128)(2,1)}, bf16[128,4,4,16]{0,3,2,1:T(8,128)(2,1)S(1)}, u32[]{:S(2)}) copy-start(bf16[128,4,4,16]{0,3,2,1:T(8,128)(2,1)S(1)} %get-tuple-element.826) | copy-start | bytes 196612
  49.0 38.5 %copy-start.23 = (bf16[128,4,4,16]{0,3,2,1:T(8,128)(2,1)}, bf16[128,4,4,16]{0,3,2,1:T(8,128)(2,1)S(1)}, u32[]{:S(2)}) copy-start(bf16[128,4,4,16]{0,3,2,1:T(8,128)(2,1)S(1)} %get-tuple-element.817) | copy-start | bytes 196612
  49.0 38.5 %copy-start.25 = (bf16[128,4,4,16]{0,3,2,1:T(8,128)(2,1)}, bf16[128,4,4,16]{0,3,2,1:T(8,128)(2,1)S(1)}, u32[]{:S(2)}) copy-start(bf16[128,4,4,16]{0,3,2,1:T(8,128)(2,1)S(1)} %get-tuple-element.818) | copy-start | bytes 196612
  88.1 15.3 %collective-permute-start = (bf16[2,128,4,256]{1,3,2,0:T(8,128)(2,1)}, bf16[2,128,4,256]{1,3,2,0:T(8,128)(2,1)S(1)}, u32[]{:S(2)}, u32[]{:S(2)}) collective-permute-start(bf16[2,128,4,256]{1,3,2,0:T(8,128)(2,1)} %get-tuple-element.1023), channel_id=1, source_target_pairs={{0,8},{8,16},{16,24},{1,9},{9,17},{17,25},{2,10},{10,18},{18,26},{... | collective-permute-start | bytes 1572872 | tf_op jit(solution)/shard_map/while/body/eval_jaxpr/ppermute | solution.py:21
  104.7 15.3 %collective-permute-start = (bf16[2,128,4,256]{1,3,2,0:T(8,128)(2,1)}, bf16[2,128,4,256]{1,3,2,0:T(8,128)(2,1)S(1)}, u32[]{:S(2)}, u32[]{:S(2)}) collective-permute-start(bf16[2,128,4,256]{1,3,2,0:T(8,128)(2,1)} %get-tuple-element.1023), channel_id=1, source_target_pairs={{0,8},{8,16},{16,24},{1,9},{9,17},{17,25},{2,10},{10,18},{18,26},{... | collective-permute-start | bytes 1572872 | tf_op jit(solution)/shard_map/while/body/eval_jaxpr/ppermute | solution.py:21
  121.4 14.4 %collective-permute-start = (bf16[2,128,4,256]{1,3,2,0:T(8,128)(2,1)}, bf16[2,128,4,256]{1,3,2,0:T(8,128)(2,1)S(1)}, u32[]{:S(2)}, u32[]{:S(2)}) collective-permute-start(bf16[2,128,4,256]{1,3,2,0:T(8,128)(2,1)} %get-tuple-element.1023), channel_id=1, source_target_pairs={{0,8},{8,16},{16,24},{1,9},{9,17},{17,25},{2,10},{10,18},{18,26},{... | collective-permute-start | bytes 1572872 | tf_op jit(solution)/shard_map/while/body/eval_jaxpr/ppermute | solution.py:21
  140.0 13.6 %collective-permute-start.1 = (bf16[2,128,4,256]{1,3,2,0:T(8,128)(2,1)}, bf16[2,128,4,256]{1,3,2,0:T(8,128)(2,1)S(1)}, u32[]{:S(2)}, u32[]{:S(2)}) collective-permute-start(bf16[2,128,4,256]{1,3,2,0:T(8,128)(2,1)} %get-tuple-element.1059), channel_id=1, source_target_pairs={{0,8},{8,16},{16,24},{1,9},{9,17},{17,25},{2,10},{10,18},{18,26},{... | collective-permute-start | bytes 1572872 | tf_op jit(solution)/shard_map/while/body/eval_jaxpr/ppermute | solution.py:21
  157.9 12.7 %collective-permute-start.1 = (bf16[2,128,4,256]{1,3,2,0:T(8,128)(2,1)}, bf16[2,128,4,256]{1,3,2,0:T(8,128)(2,1)S(1)}, u32[]{:S(2)}, u32[]{:S(2)}) collective-permute-start(bf16[2,128,4,256]{1,3,2,0:T(8,128)(2,1)} %get-tuple-element.1059), channel_id=1, source_target_pairs={{0,8},{8,16},{16,24},{1,9},{9,17},{17,25},{2,10},{10,18},{18,26},{... | collective-permute-start | bytes 1572872 | tf_op jit(solution)/shard_map/while/body/eval_jaxpr/ppermute | solution.py:21
  174.9 11.9 collective-permute-start.1
  200.0 22.8 %collective-permute-start.4 = (f32[2,128,4,256]{1,3,2,0:T(8,128)}, f32[2,128,4,256]{1,3,2,0:T(8,128)S(1)}, u32[]{:S(2)}, u32[]{:S(2)}) collective-permute-start(f32[2,128,4,256]{1,3,2,0:T(8,128)} %pad_maximum_fusion.1), channel_id=1, source_target_pairs={{0,8},{8,16},{16,24},{24,0},{1,9},{9,17},{17,25},{25,1},{2,10},{10... | collective-permute-start | bytes 3145736 | tf_op jit(solution)/shard_map/ppermute | solution.py:26
  212.5 193.8 %reduce-scatter.2.cloned.1.call-start = ((), (), s32[]{:S(2)}) async-start(), calls=%async_computation.3 | async-start | bytes 4718592 | tf_op jit(solution)/shard_map/reduce_scatter | solution.py:293
  222.8 11.2 collective-permute-start.2
  236.5 21.4 %collective-permute-start.3 = (f32[2,128,4,256]{1,3,2,0:T(8,128)S(1)}, f32[2,128,4,256]{1,3,2,0:T(8,128)S(1)}, u32[]{:S(2)}, u32[]{:S(2)}) collective-permute-start(f32[2,128,4,256]{1,3,2,0:T(8,128)S(1)} %maximum_add_fusion.2), channel_id=1, source_target_pairs={{0,8},{8,16},{16,24},{24,0},{1,9},{9,17},{17,25},{25,1},{2,10},{10... | collective-permute-start | bytes 3145736 | tf_op jit(solution)/shard_map/while/body/eval_jaxpr/ppermute | solution.py:26
  257.8 14.0 %collective-permute-start.2 = (bf16[2,128,4,256]{1,3,2,0:T(8,128)(2,1)S(1)}, bf16[2,128,4,256]{1,3,2,0:T(8,128)(2,1)S(1)}, u32[]{:S(2)}, u32[]{:S(2)}) collective-permute-start(bf16[2,128,4,256]{1,3,2,0:T(8,128)(2,1)S(1)} %get-tuple-element.1098), channel_id=1, source_target_pairs={{0,8},{8,16},{16,24},{1,9},{9,17},{17,25},{2,10},{10,18},{18,26},{... | collective-permute-start | bytes 1572872 | tf_op jit(solution)/shard_map/while/body/eval_jaxpr/ppermute | solution.py:21
  274.3 21.4 %collective-permute-start.3 = (f32[2,128,4,256]{1,3,2,0:T(8,128)S(1)}, f32[2,128,4,256]{1,3,2,0:T(8,128)S(1)}, u32[]{:S(2)}, u32[]{:S(2)}) collective-permute-start(f32[2,128,4,256]{1,3,2,0:T(8,128)S(1)} %maximum_add_fusion.2), channel_id=1, source_target_pairs={{0,8},{8,16},{16,24},{24,0},{1,9},{9,17},{17,25},{25,1},{2,10},{10... | collective-permute-start | bytes 3145736 | tf_op jit(solution)/shard_map/while/body/eval_jaxpr/ppermute | solution.py:26
  295.7 15.9 %collective-permute-start.2 = (bf16[2,128,4,256]{1,3,2,0:T(8,128)(2,1)S(1)}, bf16[2,128,4,256]{1,3,2,0:T(8,128)(2,1)S(1)}, u32[]{:S(2)}, u32[]{:S(2)}) collective-permute-start(bf16[2,128,4,256]{1,3,2,0:T(8,128)(2,1)S(1)} %get-tuple-element.1098), channel_id=1, source_target_pairs={{0,8},{8,16},{16,24},{1,9},{9,17},{17,25},{2,10},{10,18},{18,26},{... | collective-permute-start | bytes 1572872 | tf_op jit(solution)/shard_map/while/body/eval_jaxpr/ppermute | solution.py:21
  314.0 17.1 %collective-permute-start.3 = (f32[2,128,4,256]{1,3,2,0:T(8,128)S(1)}, f32[2,128,4,256]{1,3,2,0:T(8,128)S(1)}, u32[]{:S(2)}, u32[]{:S(2)}) collective-permute-start(f32[2,128,4,256]{1,3,2,0:T(8,128)S(1)} %maximum_add_fusion.2), channel_id=1, source_target_pairs={{0,8},{8,16},{16,24},{24,0},{1,9},{9,17},{17,25},{25,1},{2,10},{10... | collective-permute-start | bytes 3145736 | tf_op jit(solution)/shard_map/while/body/eval_jaxpr/ppermute | solution.py:26
  355.9 888.0 %all-reduce.9.cloned.1.call-start = ((), (), s32[]{:S(2)}) async-start(), calls=%async_computation.5 | async-start | bytes 50331648 | tf_op jit(solution)/shard_map/psum | solution.py:306
  (46 other events, 348.1 us)
Sparse Core Ops, SparseCore 0:
  12.9 30.4 all-gather.2
  45.3 27.7 all-gather.4
  212.6 79.8 all-reduce.6
  356.0 50.2 reduce-scatter.1
  410.1 833.7 all-reduce.8
where the time goes:
time: 1280 us; the launch traced here: 1270 us
  waiting for transfers between devices  966 us (75%)
  matrix products  90 us (7%)
  local copies, waits for them, and re-layouts  72 us (6%)
  blocking collectives  57.2 us (4%)
  starting transfers between devices  47.5 us (4%)
  other arithmetic  19.5 us (2%)
  between operations  15.5 us (1%)
    psum x1, waiting for transfers between devices, per_device(): lax.psum((attend_grad, attend_bias_grad, output_grad, up_grad, up_bias_gr...  788 us
    ppermute x9, waiting for transfers between devices, from_behind(): lax.ppermute(value, axis, [(source, source + steps) for source in range(l...  86.2 us
    ppermute x4, waiting for transfers between devices, from_behind_2(): lax.ppermute(value, axis, [(i, (i + by) % devices) for i in range(devices)])  52.9 us
    psum x1, blocking collectives, per_device(): norm_sums = lax.psum((gain_part, offset_part, final_part), ('seq', 'tp'))  45.8 us
    ppermute x9, starting transfers between devices, from_behind(): lax.ppermute(value, axis, [(source, source + steps) for source in range(l...  36.9 us
    unnamed x113, local copies, waits for them, and re-layouts  30.5 us
  transfers between devices with their start and end apart: 18, of which 17 were waited for; matrix products, arithmetic and copies ran while one was open for 9% of the time, Pallas kernels for 0%

commit v1 on v0

v1 whole, which is shorter than its diff:
```python
import functools
import math

import jax
import jax.numpy as jnp
from jax import lax
from jax.experimental import pallas as pl
from jax.experimental.pallas import tpu as pltpu
from jax.sharding import PartitionSpec as P

HEAD_DIM = 64
ROT = 32

EPS = 1e-05
GELU_C = 0.7978845608028654
CUBIC = 0.044715
LOG_BASE = math.log(10000.0)
BF = jnp.bfloat16
F32 = jnp.float32


def gelu_parts(pre_act):
    inner_arg = GELU_C * (pre_act + CUBIC * pre_act * pre_act * pre_act)
    tanh_value = jnp.tanh(inner_arg)
    gelu_value = 0.5 * pre_act * (1.0 + tanh_value)
    gelu_slope = 0.5 * (1.0 + tanh_value) + 0.5 * pre_act * (
        1.0 - tanh_value * tanh_value
    ) * GELU_C * (1.0 + 3.0 * CUBIC * pre_act * pre_act)
    return (gelu_value, gelu_slope)


def rotary_tables(length, width):
    half_rot = ROT // 2
    frequency = jnp.exp(jnp.arange(half_rot, dtype=F32) * (-2.0 * LOG_BASE / ROT))
    angles = jnp.arange(length, dtype=jnp.int32).astype(F32)[:, None] * frequency[None, :]
    cosine, sine = jnp.cos(angles), jnp.sin(angles)
    zero = jnp.zeros_like(sine)
    rest = jnp.zeros((length, HEAD_DIM - ROT), F32)
    own = jnp.concatenate([cosine, cosine, rest + 1.0], axis=1)
    right = jnp.concatenate([-sine, zero, rest], axis=1)
    left = jnp.concatenate([zero, sine, rest], axis=1)
    reps = (1, width // HEAD_DIM)
    return jnp.tile(own, reps), jnp.tile(right, reps), jnp.tile(left, reps)


def dot(a, b, dims, out=F32):
    return lax.dot_general(a, b, ((dims[:1], dims[1:]), ((), ())), preferred_element_type=out)


def attention_body(
    width, q_ref, k_ref, v_ref, g_ref, bq_ref, bk_ref, bv_ref, own_ref, right_ref, left_ref,
    ctx_ref, dq_ref, dk_ref, dv_ref, bias_ref,
):
    length = own_ref.shape[0]
    half = ROT // 2
    own, right, left = own_ref[...], right_ref[...], left_ref[...]

    def flat(ref):
        return ref[...].reshape(length, width)

    def rotated(x):
        return (
            x * own
            + pltpu.roll(x, width - half, 1) * right
            + pltpu.roll(x, half, 1) * left
        )

    def unrotated(x):
        return (
            x * own
            - pltpu.roll(x, width - half, 1) * right
            - pltpu.roll(x, half, 1) * left
        )

    q_all = rotated(flat(q_ref) + bq_ref[...]).astype(BF)
    k_all = rotated(flat(k_ref) + bk_ref[...]).astype(BF)
    v_all = (flat(v_ref) + bv_ref[...]).astype(BF)
    g_all = flat(g_ref)
    scale = HEAD_DIM ** (-0.5)
    block = min(256, length)
    ctx_heads, dq_heads, dk_heads, dv_heads = [], [], [], []
    for head in range(width // HEAD_DIM):
        lanes = slice(head * HEAD_DIM, (head + 1) * HEAD_DIM)
        q, k, v, g = q_all[:, lanes], k_all[:, lanes], v_all[:, lanes], g_all[:, lanes]
        ctx_rows, dq_rows = [], []
        dk = dv = None
        for start in range(0, length, block):
            stop = start + block
            qb, gb = q[start:stop], g[start:stop]
            s = dot(qb, k[:stop], (1, 1)) * scale
            row = lax.broadcasted_iota(jnp.int32, s.shape, 0) + start
            col = lax.broadcasted_iota(jnp.int32, s.shape, 1)
            s = jnp.where(row >= col, s, -jnp.inf)
            m = jnp.max(s, axis=1, keepdims=True)
            p = jnp.exp(s - m)
            p = p * (1.0 / jnp.sum(p, axis=1, keepdims=True))
            pb = p.astype(BF)
            ctx = dot(pb, v[:stop], (1, 0)).astype(BF)
            delta = jnp.sum(gb.astype(F32) * ctx.astype(F32), axis=1, keepdims=True)
            dp = dot(gb, v[:stop], (1, 1))
            ds = (p * (dp - delta) * scale).astype(BF)
            ctx_rows.append(ctx)
            dq_rows.append(dot(ds, k[:stop], (1, 0)))
            dvb = dot(pb, gb, (0, 0))
            dkb = dot(ds, qb, (0, 0))
            if start == 0:
                dk, dv = dkb, dvb
            else:
                dk = jnp.concatenate([dk + dkb[:start], dkb[start:]], axis=0)
                dv = jnp.concatenate([dv + dvb[:start], dvb[start:]], axis=0)
        ctx_heads.append(jnp.concatenate(ctx_rows, axis=0))
        dq_heads.append(jnp.concatenate(dq_rows, axis=0))
        dk_heads.append(dk)
        dv_heads.append(dv)

    def joined(parts):
        return jnp.concatenate(parts, axis=1)

    dq = unrotated(joined(dq_heads))
    dk = unrotated(joined(dk_heads))
    dv = joined(dv_heads)
    ctx_ref[...] = joined(ctx_heads).reshape(ctx_ref.shape)
    for place, (ref, value) in enumerate(((dq_ref, dq), (dk_ref, dk), (dv_ref, dv))):
        ref[...] = value.astype(BF).reshape(ref.shape)
        bias_ref[0, place : place + 1, :] = jnp.sum(value, axis=0, keepdims=True)


def attention(projected, ctx_grad, bias, devices, seqs, rows):
    local = ctx_grad.shape[1]
    width = min(128, local)
    groups = local // width
    length = devices * rows
    own, right, left = rotary_tables(length, width)
    proj4 = projected.reshape(devices, seqs, rows, 3 * local)
    grad4 = ctx_grad.reshape(devices, seqs, rows, local)

    def spec(part):
        return pl.BlockSpec((devices, None, rows, width), lambda s, h: (0, s, 0, part * groups + h))

    def bias_spec(part):
        return pl.BlockSpec((1, width), lambda s, h: (0, part * groups + h))

    table = pl.BlockSpec((length, width), lambda s, h: (0, 0))
    out4 = jax.ShapeDtypeStruct((devices, seqs, rows, local), BF)
    flat_bias = bias.reshape(1, 3 * local)
    ctx, dq, dk, dv, bias_grad = pl.pallas_call(
        functools.partial(attention_body, width),
        grid=(seqs, groups),
        in_specs=[spec(0), spec(1), spec(2), spec(0), bias_spec(0), bias_spec(1), bias_spec(2), table, table, table],
        out_specs=[spec(0)] * 4 + [pl.BlockSpec((1, 3, width), lambda s, h: (s, 0, h))],
        out_shape=[out4] * 4 + [jax.ShapeDtypeStruct((seqs, 3, local), F32)],
        name="attention",
    )(proj4, proj4, proj4, grad4, flat_bias, flat_bias, flat_bias, own, right, left)
    tokens = devices * seqs * rows
    return (
        ctx.reshape(tokens, local),
        [dq.reshape(tokens, local), dk.reshape(tokens, local), dv.reshape(tokens, local)],
        jnp.sum(bias_grad, axis=0),
    )


def per_device(
    stream,
    norm_gain,
    norm_offset,
    attend_weight,
    attend_bias,
    output_weight,
    up_weight,
    up_bias,
    down_weight,
    final_bias,
    cotangent,
):
    rows, seqs, width = stream.shape
    local = attend_weight.shape[2]
    tp = lax.axis_size("tp")
    devices = lax.axis_size("seq") * tp
    block = tp * seqs * rows

    def by_sequence(value):
        return jnp.swapaxes(value, 0, 1).reshape(seqs * rows, width)

    def by_place(value):
        return jnp.swapaxes(value.reshape(seqs, rows, width), 0, 1)

    own_stream = by_sequence(stream)
    own_cot = by_sequence(cotangent)
    row_mean = jnp.mean(own_stream, axis=-1, keepdims=True)
    centred = own_stream - row_mean
    inverse_std = lax.rsqrt(jnp.mean(centred * centred, axis=-1, keepdims=True) + EPS)
    unit_rows = centred * inverse_std
    own_normed = (unit_rows * norm_gain + norm_offset).astype(BF)
    own_grad = own_cot.astype(BF)
    normed = lax.all_gather(own_normed, ("seq", "tp"), axis=0, tiled=True)
    grads = lax.all_gather(own_grad, ("seq", "tp"), axis=0, tiled=True)

    weights = jnp.swapaxes(attend_weight, 0, 1)
    projected = jnp.concatenate(
        [dot(normed, weights[i], (1, 0)) for i in range(3)], axis=1
    )
    up_pre = dot(normed, up_weight, (1, 0)) + up_bias
    up_value, up_slope = gelu_parts(up_pre)
    hidden = up_value.astype(BF)
    ctx_grad = dot(grads, output_weight, (1, 1)).astype(BF)
    pre_grad = dot(grads, down_weight, (1, 1)) * up_slope
    up_bias_grad = jnp.sum(pre_grad, axis=0)
    pre_rounded = pre_grad.astype(BF)
    context, proj_grads, attend_bias_grad = attention(
        projected, ctx_grad, attend_bias, devices, seqs, rows
    )
    start = lax.axis_index("seq") * block

    def own_block(value):
        return lax.dynamic_slice_in_dim(value, start, block, 0)

    summed = dot(own_block(context), output_weight, (1, 0)) + dot(
        own_block(hidden), down_weight, (1, 0)
    )
    branch_total = lax.psum_scatter(summed, "tp", scatter_dimension=0, tiled=True)
    result = by_place(own_stream + branch_total + final_bias)
    back = dot(own_block(pre_rounded), up_weight, (1, 1))
    for i in range(3):
        back = back + dot(own_block(proj_grads[i]), weights[i], (1, 1))
    normed_grad = lax.psum_scatter(back, "tp", scatter_dimension=0, tiled=True)

    output_grad = dot(context, grads, (0, 0))
    down_grad = dot(hidden, grads, (0, 0))
    up_grad = dot(normed, pre_rounded, (0, 0))
    attend_grad = jnp.swapaxes(
        jnp.stack([dot(normed, part, (0, 0)) for part in proj_grads]), 0, 1
    )

    scaled = normed_grad * norm_gain
    stream_grad = own_cot + inverse_std * (
        scaled
        - jnp.mean(scaled, axis=-1, keepdims=True)
        - unit_rows * jnp.mean(scaled * unit_rows, axis=-1, keepdims=True)
    )
    sums = jnp.stack(
        [
            jnp.sum(normed_grad * unit_rows, axis=0),
            jnp.sum(normed_grad, axis=0),
            jnp.sum(own_cot, axis=0),
        ]
    )
    sums = lax.psum(sums, ("seq", "tp"))
    return (
        result,
        by_place(stream_grad),
        sums[0],
        sums[1],
        attend_grad,
        attend_bias_grad,
        output_grad,
        up_grad,
        up_bias_grad,
        down_grad,
        sums[2],
    )


def solution(mesh):
    in_specs = (
        P(("seq", "tp"), None, None),
        P(),
        P(),
        P(None, None, "tp"),
        P(None, "tp"),
        P("tp", None),
        P(None, "tp"),
        P("tp"),
        P("tp", None),
        P(),
        P(("seq", "tp"), None, None),
    )
    out_specs = (
        P(("seq", "tp"), None, None),
        P(("seq", "tp"), None, None),
        P(),
        P(),
        P(None, None, "tp"),
        P(None, "tp"),
        P("tp", None),
        P(None, "tp"),
        P("tp"),
        P("tp", None),
        P(),
    )
    return jax.shard_map(
        per_device, mesh=mesh, in_specs=in_specs, out_specs=out_specs, check_vma=False
    )
```

time: 1280 us -> 440 us (0.34)
  waiting for transfers between devices: 966 us -> 178 us
  local copies, waits for them, and re-layouts: 72 us -> 18.5 us
  starting transfers between devices: 47.5 us -> 0.16 us
  Pallas kernels: 0 us -> 39.6 us
  matrix products: 90 us -> 127 us
  blocking collectives: 57.2 us -> 39.5 us
    psum x1 -> x0, waiting for transfers between devices: 788 us -> none  [per_device(): lax.psum((attend_grad, attend_bias_grad, output_grad, up_grad, up_bias_gr...]
    ppermute x13 -> x0, waiting for transfers between devices: 139 us -> none  [the longest x9 86.2 us: from_behind(): lax.ppermute(value, axis, [(source, source + steps) for source in range(l...]
    all_gather x2, waiting for transfers between devices: 27.9 us -> 130 us  [the longest x1 72.6 us: per_device(): normed = lax.all_gather(own_normed, ('seq', 'tp'), axis=0, tiled=True)]
    ppermute x13 -> x0, starting transfers between devices: 46.9 us -> none  [the longest x9 36.9 us: from_behind(): lax.ppermute(value, axis, [(source, source + steps) for source in range(l...]
    pallas_call x0 -> x1, Pallas kernels: none -> 39.6 us  [attention(): pl.pallas_call(functools.partial(attention_body, width), grid=(seqs, grou...]
    dot_general x39 -> x18, matrix products: 90 us -> 127 us  [dot(): lax.dot_general(a, b, ((dims[:1], dims[1:]), ((), ())), preferred_element...]
    reduce_scatter x1 -> x2, waiting for transfers between devices: 11.9 us -> 48.3 us  [the longest x1 48.3 us: per_device(): lax.psum_scatter(summed, 'tp', scatter_dimension=0, tiled=True)]
    unnamed x113 -> x61, local copies, waits for them, and re-layouts: 30.5 us -> 3.21 us
  transfers between devices with their start and end apart: 18 -> 4, of which waited for: 17 -> 3; matrix products, arithmetic and copies ran while one was open for 9% -> 19% of each run, Pallas kernels for 0% -> 0%
where the time goes in v1:
time: 440 us; the launch traced here: 433 us
  waiting for transfers between devices  178 us (40%)
  matrix products  127 us (29%)
  Pallas kernels  39.6 us (9%)
  blocking collectives  39.5 us (9%)
  local copies, waits for them, and re-layouts  18.5 us (4%)
  other arithmetic  15.2 us (3%)
  between operations  14.6 us (3%)
    dot_general x18, matrix products, dot(): lax.dot_general(a, b, ((dims[:1], dims[1:]), ((), ())), preferred_element...  127 us
    all_gather x1, waiting for transfers between devices, per_device(): normed = lax.all_gather(own_normed, ('seq', 'tp'), axis=0, tiled=True)  72.6 us
    all_gather x1, waiting for transfers between devices, per_device(): grads = lax.all_gather(own_grad, ('seq', 'tp'), axis=0, tiled=True)  57.3 us
    reduce_scatter x1, waiting for transfers between devices, per_device(): lax.psum_scatter(summed, 'tp', scatter_dimension=0, tiled=True)  48.3 us
    pallas_call x1, Pallas kernels, attention(): pl.pallas_call(functools.partial(attention_body, width), grid=(seqs, grou...  39.6 us
    psum x1, blocking collectives, per_device(): sums = lax.psum(sums, ('seq', 'tp'))  39.5 us
  transfers between devices with their start and end apart: 4, of which 3 were waited for; matrix products, arithmetic and copies ran while one was open for 19% of the time, Pallas kernels for 0%

profile of v1, /device:TPU:0, one launch (start us, length us, event | category | flops | bytes accessed | tf_op | source)
XLA Modules:
  0.0 433.0 jit_solution(12577078859089115229)
XLA Ops:
  20.5 72.6 %all-gather.3.cloned.1.call-done = bf16[2048,2048]{1,0:T(8,128)(2,1)} async-done(((bf16[64,2048]{1,0:T(8,128)(2,1)}), bf16[2048,2048]{1,0:T(8,128)(2,1)}) %all-gather.3.cloned.1.call-update) | async-done | bytes 8388624 | tf_op jit(solution)/shard_map/all_gather | solution.py:195
  93.1 6.1 %fusion.14 = f32[2048,256]{0,1:T(8,128)S(1)} fusion(bf16[2048,2048]{1,0:T(8,128)(2,1)} %all-gather.3.cloned.1.call-done, bf16[3,2048,256]{2,1,0:T(8,128)(2,1)} %bitcast.103), kind=kOutput, calls=%fused_computation.28 | convolution fusion | flops 2147483648 | bytes 11534336 | tf_op jit(solution)/shard_map/dot_general | solution.py:47
  100.1 2.5 fusion.13
  102.5 2.5 fusion.11
  105.0 3.1 pad_maximum_fusion
  108.1 6.8 %copy.51 = f32[2048,768]{1,0:T(8,128)} copy(f32[2048,768]{0,1:T(8,128)} %pad_maximum_fusion) | data formatting | bytes 12582912 | tf_op jit(solution)/shard_map/concatenate | solution.py:199
  114.9 57.3 %all-gather.5.cloned.1.call-done = bf16[2048,2048]{1,0:T(8,128)(2,1)} async-done(((bf16[64,2048]{1,0:T(8,128)(2,1)}), bf16[2048,2048]{1,0:T(8,128)(2,1)}) %all-gather.5.cloned.1.call-update) | async-done | bytes 8388624 | tf_op jit(solution)/shard_map/all_gather | solution.py:196
  172.2 6.7 %convolution_convert_fusion = bf16[2048,256]{1,0:T(8,128)(2,1)} fusion(bf16[2048,2048]{1,0:T(8,128)(2,1)} %all-gather.5.cloned.1.call-done, bf16[256,2048]{1,0:T(8,128)(2,1)S(1)} %copy-done), kind=kOutput, calls=%fused_computation.16 | convolution fusion | flops 2148007936 | bytes 10485760 | tf_op jit(solution)/shard_map/dot_general | solution.py:47
  178.9 39.6 %attention.1 = (bf16[32,4,16,256]{3,2,1,0:T(8,128)(2,1)}, bf16[32,4,16,256]{3,2,1,0:T(8,128)(2,1)}, bf16[32,4,16,256]{3,2,1,0:T(8,128)(2,1)}, bf16[32,4,16,256]{3,2,1,0:T(8,128)(2,1)}, f32[4,3,256]{2,1,0:T(4,128)}) custom-call(f32[32,4,16,768]{3,2,1,0:T(8,128)} %bitcast.93, f32[32,4,16,768]{3,2,1,0:T(8,128)} %bitcast.94, f32[32,4,16,768]{3,2,1,0:T(8,128)} %bitcast.95, ...), custom_call_target="tpu_custom_call" | custom-call | tf_op jit(solution)/shard_map/attention/pallas_call | solution.py:146
  220.8 16.9 %multiply_convert_fusion = (bf16[2048,1024]{1,0:T(8,128)(2,1)}, f32[2048,1024]{1,0:T(8,128)}) fusion(f32[1024]{0:T(1024)S(1)} %copy-done.20, bf16[2048,2048]{1,0:T(8,128)(2,1)} %all-gather.3.cloned.1.call-done, bf16[2048,1024]{1,0:T(8,128)(2,1)} %param.17), kind=kOutput, calls=%fused_computation.8 | convolution fusion | flops 8610906112 | bytes 25169920 | tf_op jit(solution)/shard_map/dot_general | solution.py:47
  237.7 31.6 %fusion.28 = (f32[1024]{0:T(1024)}, bf16[2048,1024]{1,0:T(8,128)(2,1)}) fusion(f32[2048,1024]{1,0:T(8,128)} %get-tuple-element.39, f32[1024]{0:T(1024)S(1)} %copy-done.20, bf16[2048,2048]{1,0:T(8,128)(2,1)S(1)} %bitcast.97, bf16[1024,2048]{1,0:T(8,128)(2,1)} %param.19), kind=kOutput, calls=%fused_computation.66 | convolution fusion | flops 8633973760 | bytes 25174016 | tf_op jit(solution)/shard_map/dot_general | solution.py:47
  269.2 3.7 fusion.6
  273.8 3.9 add_add_fusion
  278.5 4.9 %fusion.8 = f32[512,2048]{1,0:T(8,128)S(1)} fusion(bf16[1024,2048]{1,0:T(8,128)(2,1)} %param.19, bf16[2048,1024]{1,0:T(8,128)(2,1)} %get-tuple-element.38, s32[]{:T(128)S(6)} %select_n.2), kind=kOutput, calls=%fused_computation.22 | convolution fusion | flops 2147483648 | bytes 9437188 | tf_op jit(solution)/shard_map/dot_general | solution.py:47
  283.4 2.8 convolution_add_fusion
  286.3 7.0 %convolution_bitcast_fusion = f32[1,2048,256]{2,1,0:T(8,128)S(1)} fusion(bf16[2048,2048]{1,0:T(8,128)(2,1)} %all-gather.3.cloned.1.call-done, bf16[2048,256]{1,0:T(8,128)(2,1)} %bitcast.123), kind=kOutput, calls=%fused_computation.13 | convolution fusion | flops 2147483648 | bytes 11534336 | tf_op jit(solution)/shard_map/dot_general | solution.py:47
  293.3 6.2 %convolution_bitcast_fusion.1 = f32[1,2048,256]{2,1,0:T(8,128)S(1)} fusion(bf16[2048,2048]{1,0:T(8,128)(2,1)} %all-gather.3.cloned.1.call-done, bf16[2048,256]{1,0:T(8,128)(2,1)S(1)} %bitcast.121), kind=kOutput, calls=%fused_computation.14 | convolution fusion | flops 2147483648 | bytes 11534336 | tf_op jit(solution)/shard_map/dot_general | solution.py:47
  299.5 2.6 convolution_bitcast_fusion.2
  302.2 3.1 maximum_bitcast_fusion
  305.3 3.9 fusion.30
  309.2 11.5 %fusion.31 = f32[2048,1024]{1,0:T(8,128)} fusion(bf16[2048,2048]{1,0:T(8,128)(2,1)S(1)} %bitcast.135, bf16[2048,1024]{1,0:T(8,128)(2,1)S(1)} %copy-done.21), kind=kOutput, calls=%fused_computation.69 | convolution fusion | flops 8589934592 | bytes 20971520 | tf_op jit(solution)/shard_map/dot_general | solution.py:47
  320.8 11.5 %fusion.32 = f32[1024,2048]{1,0:T(8,128)} fusion(bf16[2048,1024]{1,0:T(8,128)(2,1)S(1)} %copy-done.22, bf16[2048,2048]{1,0:T(8,128)(2,1)S(1)} %bitcast.99), kind=kOutput, calls=%fused_computation.70 | convolution fusion | flops 8589934592 | bytes 20971520 | tf_op jit(solution)/shard_map/dot_general | solution.py:47
  333.8 48.3 %reduce-scatter.3.cloned.1.call-done = f32[64,2048]{1,0:T(8,128)} async-done(((f32[512,2048]{1,0:T(8,128)}), f32[64,2048]{1,0:T(8,128)}) %reduce-scatter.3.cloned.1.call-update) | async-done | bytes 524304 | tf_op jit(solution)/shard_map/reduce_scatter | solution.py:220
  386.0 39.5 %psum.7 = f32[3,2048]{1,0:T(4,128)S(1)} all-reduce(f32[3,2048]{1,0:T(4,128)S(1)} %pad_maximum_fusion.1), channel_id=1, replica_groups=mesh['seq'=4,'tp'=8] {'seq','tp'}, use_global_device_ids=true, to_apply=%region_9.0 | all-reduce | flops 6144 | bytes 49152 | tf_op jit(solution)/shard_map/psum | solution.py:247
  (110 shorter events, 23.8 us)
Async XLA Ops:
  7.2 165.0 %copy-start = (bf16[256,2048]{1,0:T(8,128)(2,1)S(1)}, bf16[256,2048]{1,0:T(8,128)(2,1)}, u32[]{:S(2)}) copy-start(bf16[256,2048]{1,0:T(8,128)(2,1)} %param.16) | copy-start | bytes 3145732
  7.2 85.9 %all-gather.3.cloned.1.call-start = ((), (), s32[]{:S(2)}) async-start(), calls=%async_computation.2 | async-start | bytes 8650752 | tf_op jit(solution)/shard_map/all_gather | solution.py:195
  11.3 87.9 %copy-start.1 = (f32[4,16,2048]{2,1,0:T(8,128)}, f32[4,16,2048]{2,1,0:T(8,128)S(1)}, u32[]{:S(2)}) copy-start(f32[4,16,2048]{2,1,0:T(8,128)S(1)} %copy.47) | copy-start | bytes 1572868
  11.5 6.1 %copy-start.14 = (f32[64]{0:T(128)}, f32[64]{0:T(128)S(1)}, u32[]{:S(2)}) copy-start(f32[64]{0:T(128)S(1)} %rsqrt.12) | copy-start | bytes 772
  13.1 159.1 %all-gather.5.cloned.1.call-start = ((), (), s32[]{:S(2)}) async-start(), calls=%async_computation.3 | async-start | bytes 8650752 | tf_op jit(solution)/shard_map/all_gather | solution.py:196
  16.1 316.2 %reduce-scatter.5.cloned.1.call-start = ((), (), s32[]{:S(2)}) async-start(), calls=%async_computation.5 | async-start | bytes 4718592 | tf_op jit(solution)/shard_map/reduce_scatter | solution.py:225
  93.1 6.2 %copy-start.6 = (bf16[2048,3,256]{2,0,1:T(8,128)(2,1)S(1)}, bf16[2048,3,256]{2,0,1:T(8,128)(2,1)}, u32[]{:S(2)}) copy-start(bf16[2048,3,256]{2,0,1:T(8,128)(2,1)} %param.14) | copy-start | bytes 9437188
  93.1 7.0 %copy-start.18 = (bf16[2048,2048]{1,0:T(8,128)(2,1)S(1)}, bf16[2048,2048]{1,0:T(8,128)(2,1)}, u32[]{:S(2)}) copy-start(bf16[2048,2048]{1,0:T(8,128)(2,1)} %all-gather.3.cloned.1.call-done) | copy-start | bytes 25165828
  178.9 41.8 %copy-start.20 = (f32[1024]{0:T(1024)S(1)}, f32[1024]{0:T(1024)}, u32[]{:S(2)}) copy-start(f32[1024]{0:T(1024)} %param.18) | copy-start | bytes 12292
  218.5 19.1 %slice-start = ((s8[8388608]{0:T(1024)(128)(4,1)}), s8[4194304]{0:T(1024)(128)(4,1)S(1)}, s32[]{:S(2)}) async-start(s8[8388608]{0:T(1024)(128)(4,1)} %bitcast.96), calls=%async_computation.6 | async-start | bytes 8388608
  220.8 16.9 %slice-start.1 = ((s8[8388608]{0:T(1024)(128)(4,1)}), s8[4194304]{0:T(1024)(128)(4,1)S(1)}, s32[]{:S(2)}) async-start(s8[8388608]{0:T(1024)(128)(4,1)} %bitcast.96), calls=%async_computation.7 | async-start | bytes 8388608
  237.6 31.6 %copy-start.19 = (bf16[2048,1024]{1,0:T(8,128)(2,1)S(1)}, bf16[2048,1024]{1,0:T(8,128)(2,1)}, u32[]{:S(2)}) copy-start(bf16[2048,1024]{1,0:T(8,128)(2,1)} %param.17) | copy-start | bytes 12582916
  277.7 104.3 %reduce-scatter.3.cloned.1.call-start = ((), (), s32[]{:S(2)}) async-start(), calls=%async_computation.4 | async-start | bytes 4718592 | tf_op jit(solution)/shard_map/reduce_scatter | solution.py:220
  286.2 7.1 %copy-start.11 = (bf16[32,4,16,256]{3,2,1,0:T(8,128)(2,1)S(1)}, bf16[32,4,16,256]{3,2,1,0:T(8,128)(2,1)}, u32[]{:S(2)}) copy-start(bf16[32,4,16,256]{3,2,1,0:T(8,128)(2,1)} %get-tuple-element.18) | copy-start | bytes 3145732
  286.2 13.3 %slice-start.4 = ((s8[8388608]{0:T(1024)(128)(4,1)}), s8[4194304]{0:T(1024)(128)(4,1)S(1)}, s32[]{:S(2)}) async-start(s8[8388608]{0:T(1024)(128)(4,1)} %bitcast.134), calls=%async_computation.10 | async-start | bytes 8388608
  293.3 6.2 %slice-start.5 = ((s8[8388608]{0:T(1024)(128)(4,1)}), s8[4194304]{0:T(1024)(128)(4,1)S(1)}, s32[]{:S(2)}) async-start(s8[8388608]{0:T(1024)(128)(4,1)} %bitcast.134), calls=%async_computation.11 | async-start | bytes 8388608
  293.3 11.9 %slice-start.2 = ((s8[8388608]{0:T(1024)(128)(4,1)}), s8[4194304]{0:T(1024)(128)(4,1)S(1)}, s32[]{:S(2)}) async-start(s8[8388608]{0:T(1024)(128)(4,1)} %bitcast.98), calls=%async_computation.8 | async-start | bytes 8388608
  309.2 11.6 %copy-start.22 = (bf16[2048,1024]{1,0:T(8,128)(2,1)S(1)}, bf16[2048,1024]{1,0:T(8,128)(2,1)}, u32[]{:S(2)}) copy-start(bf16[2048,1024]{1,0:T(8,128)(2,1)} %get-tuple-element.38) | copy-start | bytes 12582916
  320.8 11.6 %copy-start.2 = (f32[4,16,2048]{2,1,0:T(8,128)S(1)}, f32[4,16,2048]{2,1,0:T(8,128)}, u32[]{:S(2)}) copy-start(f32[4,16,2048]{2,1,0:T(8,128)} %copy-done.1) | copy-start | bytes 1572868
  320.8 11.6 %copy-start.9 = (f32[2048]{0:T(1024)S(1)}, f32[2048]{0:T(1024)}, u32[]{:S(2)}) copy-start(f32[2048]{0:T(1024)} %param.12) | copy-start | bytes 24580
  320.8 11.6 %copy-start.15 = (f32[64]{0:T(128)S(1)}, f32[64]{0:T(128)}, u32[]{:S(2)}) copy-start(f32[64]{0:T(128)} %copy-done.14) | copy-start | bytes 772
  320.8 11.6 %copy-start.17 = (f32[64]{0:T(128)S(1)}, f32[64]{0:T(128)}, u32[]{:S(2)}) copy-start(f32[64]{0:T(128)} %copy-done.16) | copy-start | bytes 772
  320.8 61.3 %copy-start.4 = (f32[4,16,2048]{2,1,0:T(8,128)S(1)}, f32[4,16,2048]{2,1,0:T(8,128)}, u32[]{:S(2)}) copy-start(f32[4,16,2048]{2,1,0:T(8,128)} %copy-done.3) | copy-start | bytes 1572868
  320.8 61.2 %copy-start.13 = (f32[2048]{0:T(1024)S(1)}, f32[2048]{0:T(1024)}, u32[]{:S(2)}) copy-start(f32[2048]{0:T(1024)} %param.20) | copy-start | bytes 24580
  (9 other events, 37.0 us)
Sparse Core Ops, SparseCore 0:
  13.3 79.7 all-gather.2
  96.5 75.6 all-gather.4
  277.8 49.7 reduce-scatter.4
  330.9 51.1 reduce-scatter.2

commit v2 on v1

v2 whole, which is shorter than its diff:
```python
import functools
import math

import jax
import jax.numpy as jnp
from jax import lax
from jax.experimental import pallas as pl
from jax.experimental.pallas import tpu as pltpu
from jax.sharding import PartitionSpec as P

HEAD_DIM = 64
ROT = 32

EPS = 1e-05
GELU_C = 0.7978845608028654
CUBIC = 0.044715
LOG_BASE = math.log(10000.0)
BF = jnp.bfloat16
F32 = jnp.float32
MESH = pl.DeviceIdType.MESH


def gelu_parts(pre_act):
    inner_arg = GELU_C * (pre_act + CUBIC * pre_act * pre_act * pre_act)
    tanh_value = jnp.tanh(inner_arg)
    gelu_value = 0.5 * pre_act * (1.0 + tanh_value)
    gelu_slope = 0.5 * (1.0 + tanh_value) + 0.5 * pre_act * (
        1.0 - tanh_value * tanh_value
    ) * GELU_C * (1.0 + 3.0 * CUBIC * pre_act * pre_act)
    return (gelu_value, gelu_slope)


def dot(a, b, dims):
    return lax.dot_general(a, b, ((dims[:1], dims[1:]), ((), ())), preferred_element_type=F32)


def flip(index, bit):
    return index + bit - 2 * bit * ((index // bit) % 2)


def head_pass(q_all, k_all, v_all, g_all, heads):
    length = q_all.shape[0]
    scale = HEAD_DIM ** (-0.5)
    block = min(256, length)
    results = ([], [], [], [])
    for head in range(heads):
        lanes = slice(head * HEAD_DIM, (head + 1) * HEAD_DIM)
        q, k, v, g = q_all[:, lanes], k_all[:, lanes], v_all[:, lanes], g_all[:, lanes]
        ctx_rows, dq_rows = [], []
        dk = dv = None
        for start in range(0, length, block):
            stop = start + block
            qb, gb = q[start:stop], g[start:stop]
            s = dot(qb, k[:stop], (1, 1)) * scale
            row = lax.broadcasted_iota(jnp.int32, s.shape, 0) + start
            col = lax.broadcasted_iota(jnp.int32, s.shape, 1)
            s = jnp.where(row >= col, s, -jnp.inf)
            m = jnp.max(s, axis=1, keepdims=True)
            p = jnp.exp(s - m)
            p = p * (1.0 / jnp.sum(p, axis=1, keepdims=True))
            pb = p.astype(BF)
            ctx = dot(pb, v[:stop], (1, 0)).astype(BF)
            delta = jnp.sum(gb.astype(F32) * ctx.astype(F32), axis=1, keepdims=True)
            dp = dot(gb, v[:stop], (1, 1))
            ds = (p * (dp - delta) * scale).astype(BF)
            ctx_rows.append(ctx)
            dq_rows.append(dot(ds, k[:stop], (1, 0)))
            dvb = dot(pb, gb, (0, 0))
            dkb = dot(ds, qb, (0, 0))
            if start == 0:
                dk, dv = dkb, dvb
            else:
                dk = jnp.concatenate([dk + dkb[:start], dkb[start:]], axis=0)
                dv = jnp.concatenate([dv + dvb[:start], dvb[start:]], axis=0)
        results[0].append(jnp.concatenate(ctx_rows, axis=0))
        results[1].append(jnp.concatenate(dq_rows, axis=0))
        results[2].append(dk)
        results[3].append(dv)
    return [jnp.concatenate(parts, axis=1) for parts in results]


def block_kernel(
    dims,
    stream_ref, cot_ref, gain_ref, offset_ref, fbias_ref, abias_ref, ubias_ref,
    wa_hbm, wo_hbm, wu_hbm, wd_hbm,
    norm_out, grad_out, hid_out, pre_out, ctx_out, dproj_out,
    result_ref, sgrad_ref, sums_ref, abg_ref, ubg_ref,
    gat, wa, wo, wu, wd, unit, istd, table, proj, cgrad, hid, pre, ctx, dproj,
    part, parts_in, sum_tp, sum_seq,
    zs, zr, xs, xr, fs, fr, ps, pr, ms, mr, ws, os,
):
    Z, TP, S, R, D = dims
    z, t = lax.axis_index("seq"), lax.axis_index("tp")
    chip, core = t // 2, t % 2
    chips = TP // 2
    levels = chips.bit_length() - 1
    bits = [
        (1 - core) * (1 << i) + core * (1 << (levels - 1 - i)) for i in range(levels)
    ]
    partner = chip * 2 + 1 - core
    L = Z * TP * R
    local = wo.shape[0]
    hidden = wu.shape[1]
    pair = min(128, local)
    own_rows = TP * R

    loads = [
        pltpu.make_async_copy(src, dst, ws.at[i])
        for i, (src, dst) in enumerate(((wa_hbm, wa), (wo_hbm, wo), (wu_hbm, wu), (wd_hbm, wd)))
    ]
    for load in loads:
        load.start()
    barrier = pltpu.get_barrier_semaphore()
    for d in range(1, TP):
        pl.semaphore_signal(barrier, inc=1, device_id={"tp": (t + d) % TP}, device_id_type=MESH)
    for d in range(1, Z):
        pl.semaphore_signal(barrier, inc=1, device_id={"seq": (z + d) % Z}, device_id_type=MESH)

    @pl.loop(0, S)
    def _(s):
        x = stream_ref[:, pl.ds(s, 1), :].reshape(R, D)
        mean = jnp.mean(x, axis=-1, keepdims=True)
        centred = x - mean
        inv = lax.rsqrt(jnp.mean(centred * centred, axis=-1, keepdims=True) + EPS)
        u = centred * inv
        unit[s] = u
        istd[s] = jnp.broadcast_to(inv, (R, 128))
        gat[0, s, z, t] = (u * gain_ref[...] + offset_ref[...]).astype(BF)
        gat[1, s, z, t] = cot_ref[:, pl.ds(s, 1), :].reshape(R, D).astype(BF)

    pl.semaphore_wait(barrier, TP + Z - 2)

    def remote(src, dst, ssem, rsem, dev):
        return pltpu.make_async_remote_copy(
            src_ref=src, dst_ref=dst, send_sem=ssem, recv_sem=rsem,
            device_id=dev, device_id_type=MESH,
        )

    def same(ref, ssem, rsem, dev):
        return remote(ref, ref, ssem, rsem, dev)

    def unit_of(s, zz, tt):
        return gat.at[:, s, zz, tt]

    def column(s, tt):
        return gat.at[:, s, :, tt]

    here = {"tp": t}

    def z_copy(s, d):
        return same(unit_of(s, z, t), zs.at[s, d], zr.at[s, z], {"seq": (z + d) % Z})

    def z_sends(s):
        for d in range(1, Z):
            z_copy(s, d).start()

    def x_copy(s, d, i):
        return same(
            unit_of(s, (z + d) % Z, t), xs.at[s, i, d],
            xr.at[s, t, 0 if d == 0 else 1], {"tp": flip(chip, bits[i]) * 2 + core},
        )

    def f_copy(s, src, slot, to):
        return same(column(s, src), fs.at[s, slot], fr.at[s, src], {"tp": to})

    def source(r):
        c = chip
        for i in range(levels):
            if (r >> i) & 1:
                c = flip(c, bits[i])
        return c * 2 + core

    order = sorted(range(1, chips), key=lambda r: (bin(r).count("1"), r))

    def top(r):
        return max(i for i in range(levels) if (r >> i) & 1)

    def slot_of(r, i):
        return r * (levels + 1) + i

    def own_sends(s):
        for i in range(levels):
            x_copy(s, 0, i).start()

    def z_step(s):
        for d in range(1, Z):
            zz = (z + d) % Z
            same(unit_of(s, zz, t), zs.at[s, 0], zr.at[s, zz], here).wait_recv()
        for d in range(1, Z):
            for i in range(levels):
                x_copy(s, d, i).start()
        f_copy(s, t, slot_of(0, 0), partner).start()

    def f_step(s, level):
        for r in order:
            if bin(r).count("1") != level:
                continue
            src = source(r)
            if level == 1:
                same(unit_of(s, z, src), zs.at[s, 0], xr.at[s, src, 0], here).wait_recv()
                same(
                    gat.at[:, s, pl.ds(0, Z - 1), src], zs.at[s, 0], xr.at[s, src, 1], here
                ).wait_recv()
            else:
                same(column(s, src), zs.at[s, 0], fr.at[s, src], here).wait_recv()
            for i in range(top(r) + 1, levels):
                f_copy(s, src, slot_of(r, i + 1), flip(chip, bits[i]) * 2 + core).start()
            f_copy(s, src, slot_of(r, 0), partner).start()

    def end_step(s):
        for c in range(chips):
            src = ((chip + c) % chips) * 2 + 1 - core
            same(column(s, src), zs.at[s, 0], fr.at[s, src], here).wait_recv()

    def upper_steps(s):
        for level in range(2, levels + 1):
            f_step(s, level)

    def drain_gather(s):
        for d in range(1, Z):
            z_copy(s, d).wait_send()
        for d in range(Z):
            for i in range(levels):
                x_copy(s, d, i).wait_send()
        f_copy(s, t, slot_of(0, 0), partner).wait_send()
        for r in order:
            src = source(r)
            for i in range(top(r) + 1, levels):
                f_copy(s, src, slot_of(r, i + 1), flip(chip, bits[i]) * 2 + core).wait_send()
            f_copy(s, src, slot_of(r, 0), partner).wait_send()

    def p_copy(kind, s, d):
        to = (t + d) % TP
        return remote(
            part.at[kind, s, to], parts_in.at[kind, s, t], ps.at[kind, s, d], pr.at[kind, s],
            {"tp": to},
        )

    def out_copies(s):
        return [
            pltpu.make_async_copy(src, dst, os.at[i])
            for i, (src, dst) in enumerate((
                (gat.at[0, s], norm_out.at[s]), (gat.at[1, s], grad_out.at[s]),
                (hid, hid_out.at[s]), (pre, pre_out.at[s]), (ctx, ctx_out.at[s]),
                (dproj, dproj_out.at[:, s]),
            ))
        ]

    @pl.loop(0, S)
    def _(s):
        z_sends(s)

    own_sends(0)
    if S > 1:
        own_sends(1)

    lane = lax.broadcasted_iota(jnp.int32, (L, pair), 1) % HEAD_DIM
    place = lax.broadcasted_iota(jnp.int32, (L, pair), 0).astype(F32)
    half = ROT // 2
    freq = jnp.exp((lane % half).astype(F32) * (-2.0 * LOG_BASE / ROT))
    angle = place * freq
    cosine, sine = jnp.cos(angle), jnp.sin(angle)
    table[0] = jnp.where(lane < ROT, cosine, 1.0)
    table[1] = jnp.where(lane < half, -sine, 0.0)
    table[2] = jnp.where((lane >= half) & (lane < ROT), sine, 0.0)
    abg_ref[...] = jnp.zeros_like(abg_ref)
    ubg_ref[...] = jnp.zeros_like(ubg_ref)
    for load in loads:
        load.wait()

    z_step(0)
    f_step(0, 1)
    if S > 1:
        z_step(1)
    upper_steps(0)
    end_step(0)

    def turned(x, sign):
        return (
            x * table[0]
            + sign * pltpu.roll(x, pair - half, 1) * table[1]
            + sign * pltpu.roll(x, half, 1) * table[2]
        )

    @pl.loop(0, S)
    def _(s):
        rows_n = gat[0, s].reshape(L, D)
        rows_g = gat[1, s].reshape(L, D)

        @pl.when(s > 0)
        def _():
            for copy in out_copies(s - 1):
                copy.wait()

        @pl.when(s + 2 < S)
        def _():
            own_sends(s + 2)

        @pl.loop(0, 3)
        def _(j):
            proj[j] = dot(rows_n, wa[j], (1, 0)) + abias_ref[j]

        cgrad[...] = dot(rows_g, wo[...], (1, 1)).astype(BF)

        @pl.when(s + 1 < S)
        def _():
            f_step(s + 1, 1)

        @pl.loop(0, local // pair)
        def _(h):
            lanes = pl.ds(pl.multiple_of(h * pair, pair), pair)
            q = turned(proj[0, :, lanes], 1.0).astype(BF)
            k = turned(proj[1, :, lanes], 1.0).astype(BF)
            v = proj[2, :, lanes].astype(BF)
            c, dq, dk, dv = head_pass(q, k, v, cgrad[:, lanes], pair // HEAD_DIM)
            ctx[:, lanes] = c
            for j, value in enumerate((turned(dq, -1.0), turned(dk, -1.0), dv)):
                dproj[j, :, lanes] = value.astype(BF)
                abg_ref[j : j + 1, lanes] += jnp.sum(value, axis=0, keepdims=True)

        @pl.when(s + 2 < S)
        def _():
            z_step(s + 2)

        @pl.when(s + 1 < S)
        def _():
            upper_steps(s + 1)

        tile = min(256, hidden)

        @pl.loop(0, hidden // tile)
        def _(n):
            cols = pl.ds(pl.multiple_of(n * tile, tile), tile)
            value, slope = gelu_parts(dot(rows_n, wu[:, cols], (1, 0)) + ubias_ref[:, cols])
            hid[:, cols] = value.astype(BF)
            grad = dot(rows_g, wd[cols, :], (1, 1)) * slope
            pre[:, cols] = grad.astype(BF)
            ubg_ref[:, cols] += jnp.sum(grad, axis=0, keepdims=True)

        for copy in out_copies(s):
            copy.start()

        mine = pl.ds(pl.multiple_of(z * own_rows, own_rows), own_rows)

        @pl.loop(0, D // 256)
        def _(n):
            cols = pl.ds(pl.multiple_of(n * 256, 256), 256)
            out = dot(ctx[mine, :], wo[:, cols], (1, 0)) + dot(hid[mine, :], wd[:, cols], (1, 0))
            back = dot(pre[mine, :], wu[cols, :], (1, 1))
            for j in range(3):
                back = back + dot(dproj[j, mine, :], wa[j, cols, :], (1, 1))
            part[0, s, :, :, cols] = out.astype(BF).reshape(TP, R, 256)
            part[1, s, :, :, cols] = back.astype(BF).reshape(TP, R, 256)

        for kind in range(2):
            for d in range(1, TP):
                p_copy(kind, s, d).start()

        @pl.when(s + 1 < S)
        def _():
            end_step(s + 1)

    sum_tp[t] = jnp.zeros_like(sum_tp[t])

    @pl.loop(0, S)
    def _(s):
        totals = []
        for kind in range(2):
            remote(
                part.at[kind, s, pl.ds(0, TP - 1)], parts_in.at[kind, s, pl.ds(0, TP - 1)],
                ps.at[kind, s, 0], pr.at[kind, s], here,
            ).wait_recv()
            total = part[kind, s, t].astype(F32)
            for d in range(1, TP):
                total = total + parts_in[kind, s, (t + d) % TP].astype(F32)
            totals.append(total)
        branch, ngrad = totals
        x = stream_ref[:, pl.ds(s, 1), :].reshape(R, D)
        cot = cot_ref[:, pl.ds(s, 1), :].reshape(R, D)
        result_ref[:, pl.ds(s, 1), :] = (x + branch + fbias_ref[...]).reshape(R, 1, D)
        u = unit[s]
        scaled = ngrad * gain_ref[...]
        sgrad_ref[:, pl.ds(s, 1), :] = (
            cot
            + istd[s][:, :1]
            * (
                scaled
                - jnp.mean(scaled, axis=-1, keepdims=True)
                - u * jnp.mean(scaled * u, axis=-1, keepdims=True)
            )
        ).reshape(R, 1, D)
        for i, value in enumerate((ngrad * u, ngrad, cot)):
            sum_tp[t, i : i + 1, :] += jnp.sum(value, axis=0, keepdims=True)

    def m_copy(d):
        return remote(sum_tp.at[t], sum_tp.at[t], ms.at[d], mr.at[0], {"tp": (t + d) % TP})

    def n_copy(d):
        return remote(
            sum_seq.at[z], sum_seq.at[z], ms.at[TP + d], mr.at[1], {"seq": (z + d) % Z}
        )

    for d in range(1, TP):
        m_copy(d).start()
    same(sum_tp.at[pl.ds(0, TP - 1)], ms.at[0], mr.at[0], here).wait_recv()
    total = sum_tp[0]
    for d in range(1, TP):
        total = total + sum_tp[d]
    sum_seq[z] = total
    for d in range(1, Z):
        n_copy(d).start()
    same(sum_seq.at[pl.ds(0, Z - 1)], ms.at[0], mr.at[1], here).wait_recv()
    total = sum_seq[0]
    for d in range(1, Z):
        total = total + sum_seq[d]
    sums_ref[...] = total

    for d in range(1, TP):
        m_copy(d).wait_send()
    for d in range(1, Z):
        n_copy(d).wait_send()
    for copy in out_copies(S - 1):
        copy.wait()

    @pl.loop(0, S)
    def _(s):
        drain_gather(s)
        for kind in range(2):
            for d in range(1, TP):
                p_copy(kind, s, d).wait_send()


def block_call(stream, cotangent, gain, offset, fbias, abias, ubias, wa, wo, wu, wd, Z, TP):
    R, S, D = stream.shape
    local, hidden = wo.shape[0], wu.shape[1]
    L = Z * TP * R
    chips = TP // 2
    levels = chips.bit_length() - 1
    vm = pl.BlockSpec(memory_space=pltpu.VMEM)
    anywhere = pl.BlockSpec(memory_space=pl.ANY)
    shape = jax.ShapeDtypeStruct
    dma = pltpu.SemaphoreType.DMA
    return pl.pallas_call(
        functools.partial(block_kernel, (Z, TP, S, R, D)),
        in_specs=[vm] * 7 + [anywhere] * 4,
        out_specs=[anywhere] * 6 + [vm] * 5,
        out_shape=[
            shape((S, Z, TP, R, D), BF),
            shape((S, Z, TP, R, D), BF),
            shape((S, L, hidden), BF),
            shape((S, L, hidden), BF),
            shape((S, L, local), BF),
            shape((3, S, L, local), BF),
            shape((R, S, D), F32),
            shape((R, S, D), F32),
            shape((8, D), F32),
            shape((3, local), F32),
            shape((1, hidden), F32),
        ],
        scratch_shapes=[
            pltpu.VMEM((2, S, Z, TP, R, D), BF),
            pltpu.VMEM((3, D, local), BF),
            pltpu.VMEM((local, D), BF),
            pltpu.VMEM((D, hidden), BF),
            pltpu.VMEM((hidden, D), BF),
            pltpu.VMEM((S, R, D), F32),
            pltpu.VMEM((S, R, 128), F32),
            pltpu.VMEM((3, L, min(128, local)), F32),
            pltpu.VMEM((3, L, local), F32),
            pltpu.VMEM((L, local), BF),
            pltpu.VMEM((L, hidden), BF),
            pltpu.VMEM((L, hidden), BF),
            pltpu.VMEM((L, local), BF),
            pltpu.VMEM((3, L, local), BF),
            pltpu.VMEM((2, S, TP, R, D), BF),
            pltpu.VMEM((2, S, TP, R, D), BF),
            pltpu.VMEM((TP, 8, D), F32),
            pltpu.VMEM((Z, 8, D), F32),
            dma((S, Z)),
            dma((S, Z)),
            dma((S, levels, Z)),
            dma((S, TP, 2)),
            dma((S, chips * (levels + 1))),
            dma((S, TP)),
            dma((2, S, TP)),
            dma((2, S)),
            dma((TP + Z,)),
            dma((2,)),
            dma((4,)),
            dma((6,)),
        ],
        compiler_params=pltpu.CompilerParams(
            collective_id=0, has_side_effects=True, vmem_limit_bytes=67000000
        ),
        name="block",
    )(stream, cotangent, gain, offset, fbias, abias, ubias, wa, wo, wu, wd)


def per_device(
    stream,
    norm_gain,
    norm_offset,
    attend_weight,
    attend_bias,
    output_weight,
    up_weight,
    up_bias,
    down_weight,
    final_bias,
    cotangent,
):
    R, S, D = stream.shape
    local = attend_weight.shape[2]
    hidden = up_weight.shape[1]
    TP, Z = lax.axis_size("tp"), lax.axis_size("seq")
    tokens = R * S * TP * Z
    weights = jnp.swapaxes(attend_weight, 0, 1)
    (
        normed, grads, hid, pre, ctx, dproj, result, stream_grad, sums, abias_grad, ubias_grad
    ) = block_call(
        stream, cotangent, norm_gain.reshape(1, D), norm_offset.reshape(1, D),
        final_bias.reshape(1, D), attend_bias.reshape(3, 1, local), up_bias.reshape(1, hidden),
        weights, output_weight, up_weight, down_weight, Z, TP,
    )
    normed = normed.reshape(tokens, D)
    grads = grads.reshape(tokens, D)
    output_grad = dot(ctx.reshape(tokens, local), grads, (0, 0))
    down_grad = dot(hid.reshape(tokens, hidden), grads, (0, 0))
    up_grad = dot(normed, pre.reshape(tokens, hidden), (0, 0))
    attend_grad = jnp.swapaxes(
        jnp.stack([dot(normed, dproj[j].reshape(tokens, local), (0, 0)) for j in range(3)]), 0, 1
    )
    return (
        result,
        stream_grad,
        sums[0],
        sums[1],
        attend_grad,
        abias_grad,
        output_grad,
        up_grad,
        ubias_grad.reshape(hidden),
        down_grad,
        sums[2],
    )


def solution(mesh):
    in_specs = (
        P(("seq", "tp"), None, None),
        P(),
        P(),
        P(None, None, "tp"),
        P(None, "tp"),
        P("tp", None),
        P(None, "tp"),
        P("tp"),
        P("tp", None),
        P(),
        P(("seq", "tp"), None, None),
    )
    out_specs = (
        P(("seq", "tp"), None, None),
        P(("seq", "tp"), None, None),
        P(),
        P(),
        P(None, None, "tp"),
        P(None, "tp"),
        P("tp", None),
        P(None, "tp"),
        P("tp"),
        P("tp", None),
        P(),
    )
    return jax.shard_map(
        per_device, mesh=mesh, in_specs=in_specs, out_specs=out_specs, check_vma=False
    )
```

time: 440 us -> 239 us (0.54); the launches traced: 433 us -> 238 us
  waiting for transfers between devices: 178 us -> 0 us
  Pallas kernels: 39.6 us -> 188 us
  matrix products: 127 us -> 40.5 us
  blocking collectives: 39.5 us -> 0 us
  between operations: 14.6 us -> 0.74 us
  local copies, waits for them, and re-layouts: 18.5 us -> 5.86 us
  other arithmetic: 15.2 us -> 3.11 us
    pallas_call x1, Pallas kernels: 39.6 us -> 188 us  [block_call(): pl.pallas_call(functools.partial(block_kernel, (Z, TP, S, R, D)), in_spec...]
    all_gather x2 -> x0, waiting for transfers between devices: 130 us -> none  [the longest x1 72.6 us: per_device(): normed = lax.all_gather(own_normed, ('seq', 'tp'), axis=0, tiled=True)]
    dot_general x18 -> x6, matrix products: 127 us -> 40.5 us  [dot(): lax.dot_general(a, b, ((dims[:1], dims[1:]), ((), ())), preferred_element...]
    reduce_scatter x2 -> x0, waiting for transfers between devices: 48.3 us -> none  [the longest x1 48.3 us: per_device(): lax.psum_scatter(summed, 'tp', scatter_dimension=0, tiled=True)]
    psum x1 -> x0, blocking collectives: 39.5 us -> none  [per_device(): sums = lax.psum(sums, ('seq', 'tp'))]
    concatenate x3 -> x0, local copies, waits for them, and re-layouts: 6.96 us -> none  [the longest x1 6.81 us: per_device(): jnp.concatenate([dot(normed, weights[i], (1, 0)) for i in range(3)], axis=1)]
    reduce_sum x5 -> x0, other arithmetic: 4.67 us -> none  [the longest x1 1.4 us: per_device(): jnp.sum(normed_grad * unit_rows, axis=0)]
  transfers between devices with their start and end apart: 4 -> 0, of which waited for: 3 -> 0; matrix products, arithmetic and copies ran while one was open for 19% -> 0% of each run, Pallas kernels for 0% -> 0%
where the time goes in v2:
time: 239 us; the launch traced here: 238 us
  Pallas kernels  188 us (79%)
  matrix products  40.5 us (17%)
  local copies, waits for them, and re-layouts  5.86 us (2%)
  other arithmetic  3.11 us (1%)
    pallas_call x1, Pallas kernels, block_call(): pl.pallas_call(functools.partial(block_kernel, (Z, TP, S, R, D)), in_spec...  188 us
    dot_general x6, matrix products, dot(): lax.dot_general(a, b, ((dims[:1], dims[1:]), ((), ())), preferred_element...  40.5 us

profile of v2, /device:TPU:0, one launch (start us, length us, event | category | flops | bytes accessed | tf_op | source)
XLA Modules:
  0.0 238.3 jit_solution(11367982322075157560)
XLA Ops:
  0.6 1.3 reshape.58.abias_ref
  1.9 188.1 %block.1 = (bf16[4,4,8,16,2048]{4,3,2,1,0:T(8,128)(2,1)}, bf16[4,4,8,16,2048]{4,3,2,1,0:T(8,128)(2,1)}, bf16[4,512,1024]{2,1,0:T(8,128)(2,1)}, bf16[4,512,1024]{...) custom-call(f32[16,4,2048]{2,1,0:T(4,128)} %stream_ref.1, ...), custom_call_target="tpu_custom_call" | custom-call | tf_op jit(solution)/shard_map/block/pallas_call | solution.py:443
  190.0 1.6 fusion.1
  191.6 7.5 %fusion.2 = f32[256,2048]{1,0:T(8,128)} fusion(bf16[2048,256]{1,0:T(8,128)(2,1)} %bitcast.40, bf16[2048,2048]{1,0:T(8,128)(2,1)} %bitcast.37), kind=kOutput, calls=%fused_computation.6 | convolution fusion | flops 2147483648 | bytes 11534336 | tf_op jit(solution)/shard_map/dot_general | solution.py:34
  199.1 0.0 copy-done
  199.1 13.5 %fusion.4 = f32[1024,2048]{1,0:T(8,128)} fusion(bf16[2048,1024]{1,0:T(8,128)(2,1)} %bitcast.59, bf16[2048,2048]{1,0:T(8,128)(2,1)S(1)} %bitcast.38), kind=kOutput, calls=%fused_computation.8 | convolution fusion | flops 8589934592 | bytes 20971520 | tf_op jit(solution)/shard_map/dot_general | solution.py:34
  212.6 0.0 copy-done.1
  212.6 0.2 fusion
  212.8 0.0 slice-done
  212.8 0.0 slice-done.1
  212.8 2.6 %convolution_bitcast_fusion = f32[1,2048,256]{2,1,0:T(8,128)S(1)} fusion(bf16[2048,2048]{1,0:T(8,128)(2,1)S(1)} %bitcast.54, bf16[2048,256]{1,0:T(8,128)(2,1)S(1)} %bitcast.43), kind=kOutput, calls=%fused_computation.1 | convolution fusion | flops 2147483648 | bytes 11534336 | tf_op jit(solution)/shard_map/dot_general | solution.py:34
  215.4 2.6 %convolution_bitcast_fusion.2 = f32[1,2048,256]{2,1,0:T(8,128)S(1)} fusion(bf16[2048,2048]{1,0:T(8,128)(2,1)S(1)} %bitcast.55, bf16[2048,256]{1,0:T(8,128)(2,1)S(1)} %bitcast.42), kind=kOutput, calls=%fused_computation.3 | convolution fusion | flops 2147483648 | bytes 11534336 | tf_op jit(solution)/shard_map/dot_general | solution.py:34
  218.0 0.0 copy-start.6
  218.0 2.6 %convolution_bitcast_fusion.1 = f32[1,2048,256]{2,1,0:T(8,128)S(1)} fusion(bf16[2048,2048]{1,0:T(8,128)(2,1)S(1)} %bitcast.56, bf16[2048,256]{1,0:T(8,128)(2,1)S(1)} %bitcast.41), kind=kOutput, calls=%fused_computation.2 | convolution fusion | flops 2147483648 | bytes 11534336 | tf_op jit(solution)/shard_map/dot_general | solution.py:34
  220.6 0.0 copy-done.6
  220.6 11.8 %fusion.3 = f32[2048,1024]{1,0:T(8,128)} fusion(bf16[2048,2048]{1,0:T(8,128)(2,1)S(1)} %bitcast.57, bf16[2048,1024]{1,0:T(8,128)(2,1)S(1)} %bitcast.58), kind=kOutput, calls=%fused_computation.7 | convolution fusion | flops 8589934592 | bytes 20971520 | tf_op jit(solution)/shard_map/dot_general | solution.py:34
  232.4 3.1 %maximum_bitcast_fusion = f32[2048,3,256]{2,0,1:T(8,128)} fusion(f32[1,2048,256]{2,1,0:T(8,128)S(1)} %convolution_bitcast_fusion, f32[1,2048,256]{2,1,0:T(8,128)S(1)} %convolution_bitcast_fusion.1, f32[1,2048,256]{2,1,0:T(8,128)S(1)} %convolution_bitcast_fusion.2), kind=kLoop, calls=%fused_computation | loop fusion | flops 3145728 | bytes 12582912 | tf_op jit(solution)/shard_map/transpose | solution.py:530
  235.5 0.0 copy-done.3
  235.5 0.8 copy.26
  236.3 0.0 copy-done.2
  236.3 0.8 copy.27
  237.1 0.0 copy-done.5
  237.1 0.6 copy.28
  237.7 0.6 copy.29
  (10 shorter events, 0.0 us)
Async XLA Ops:
  191.6 7.5 %copy-start = (bf16[4,4,8,16,2048]{4,3,2,1,0:T(8,128)(2,1)S(1)}, bf16[4,4,8,16,2048]{4,3,2,1,0:T(8,128)(2,1)}, u32[]{:S(2)}) copy-start(bf16[4,4,8,16,2048]{4,3,2,1,0:T(8,128)(2,1)} %get-tuple-element.29) | copy-start | bytes 25165828
  191.6 21.2 %slice-start = ((s8[8388608]{0:T(1024)(128)(4,1)}), s8[4194304]{0:T(1024)(128)(4,1)S(1)}, s32[]{:S(2)}) async-start(s8[8388608]{0:T(1024)(128)(4,1)} %bitcast.52), calls=%async_computation | async-start | bytes 8388608
  199.1 13.5 %copy-start.1 = (bf16[3,4,512,256]{3,2,1,0:T(8,128)(2,1)S(1)}, bf16[3,4,512,256]{3,2,1,0:T(8,128)(2,1)}, u32[]{:S(2)}) copy-start(bf16[3,4,512,256]{3,2,1,0:T(8,128)(2,1)} %get-tuple-element.26) | copy-start | bytes 9437188
  199.1 13.7 %slice-start.1 = ((s8[8388608]{0:T(1024)(128)(4,1)}), s8[4194304]{0:T(1024)(128)(4,1)S(1)}, s32[]{:S(2)}) async-start(s8[8388608]{0:T(1024)(128)(4,1)} %bitcast.52), calls=%async_computation.1 | async-start | bytes 8388608
  218.0 2.6 %copy-start.6 = (bf16[4,512,1024]{2,1,0:T(8,128)(2,1)S(1)}, bf16[4,512,1024]{2,1,0:T(8,128)(2,1)}, u32[]{:S(2)}) copy-start(bf16[4,512,1024]{2,1,0:T(8,128)(2,1)} %get-tuple-element.30) | copy-start | bytes 12582916
  232.4 3.1 %copy-start.3 = (f32[16,4,2048]{2,1,0:T(4,128)S(1)}, f32[16,4,2048]{2,1,0:T(4,128)}, u32[]{:S(2)}) copy-start(f32[16,4,2048]{2,1,0:T(4,128)} %get-tuple-element.50) | copy-start | bytes 1572868
  232.4 3.9 %copy-start.2 = (f32[16,4,2048]{2,1,0:T(4,128)S(1)}, f32[16,4,2048]{2,1,0:T(4,128)}, u32[]{:S(2)}) copy-start(f32[16,4,2048]{2,1,0:T(4,128)} %get-tuple-element.51) | copy-start | bytes 1572868
  232.4 4.7 %copy-start.5 = (f32[3,256]{1,0:T(4,128)S(1)}, f32[3,256]{1,0:T(4,128)}, u32[]{:S(2)}) copy-start(f32[3,256]{1,0:T(4,128)} %get-tuple-element.55) | copy-start | bytes 9220
  232.4 5.3 %copy-start.4 = (f32[1,1024]{1,0:T(1,128)S(1)}, f32[1,1024]{1,0:T(1,128)}, u32[]{:S(2)}) copy-start(f32[1,1024]{1,0:T(1,128)} %get-tuple-element.31) | copy-start | bytes 12292

commit v3 on v2

--- a/solution.py
+++ b/solution.py
@@ -36,6 +36,15 @@
 
 def flip(index, bit):
     return index + bit - 2 * bit * ((index // bit) % 2)
+
+
+def flip_all(index, mask):
+    bit = 1
+    while bit <= mask:
+        if mask & bit:
+            index = flip(index, bit)
+        bit *= 2
+    return index
 
 
 def head_pass(q_all, k_all, v_all, g_all, heads):
@@ -86,8 +95,8 @@
     norm_out, grad_out, hid_out, pre_out, ctx_out, dproj_out,
     result_ref, sgrad_ref, sums_ref, abg_ref, ubg_ref,
     gat, wa, wo, wu, wd, unit, istd, table, proj, cgrad, hid, pre, ctx, dproj,
-    part, parts_in, sum_tp, sum_seq,
-    zs, zr, xs, xr, fs, fr, ps, pr, ms, mr, ws, os,
+    part, half_in, parts_in, sum_tp, sum_seq,
+    zs, zr, xs, xr, fs, fr, ps, hr, pr, ms, mr, ws, os,
 ):
     Z, TP, S, R, D = dims
     z, t = lax.axis_index("seq"), lax.axis_index("tp")
@@ -146,66 +155,65 @@
         return gat.at[:, s, :, tt]
 
     here = {"tp": t}
-
-    def z_copy(s, d):
-        return same(unit_of(s, z, t), zs.at[s, d], zr.at[s, z], {"seq": (z + d) % Z})
+    other = [z] + [flip_all(z, r) if Z & (Z - 1) == 0 else (z + r) % Z for r in range(1, Z)]
+    sender = [z] + [flip_all(z, r) if Z & (Z - 1) == 0 else (z + Z - r) % Z for r in range(1, Z)]
+
+    def z_copy(s, r):
+        return same(unit_of(s, z, t), zs.at[s, r], zr.at[s, z], {"seq": other[r]})
 
     def z_sends(s):
-        for d in range(1, Z):
-            z_copy(s, d).start()
-
-    def x_copy(s, d, i):
+        for r in range(1, Z):
+            z_copy(s, r).start()
+
+    def x_copy(s, r, src, slot, i):
         return same(
-            unit_of(s, (z + d) % Z, t), xs.at[s, i, d],
-            xr.at[s, t, 0 if d == 0 else 1], {"tp": flip(chip, bits[i]) * 2 + core},
+            unit_of(s, sender[r], src), xs.at[s, slot, r], xr.at[s, src, sender[r]],
+            {"tp": flip(chip, bits[i]) * 2 + core},
         )
 
-    def f_copy(s, src, slot, to):
-        return same(column(s, src), fs.at[s, slot], fr.at[s, src], {"tp": to})
-
-    def source(r):
+    def f_copy(s, src, r):
+        return same(column(s, src), fs.at[s, r], fr.at[s, src], {"tp": partner})
+
+    def source(mask):
         c = chip
         for i in range(levels):
-            if (r >> i) & 1:
+            if (mask >> i) & 1:
                 c = flip(c, bits[i])
         return c * 2 + core
 
-    order = sorted(range(1, chips), key=lambda r: (bin(r).count("1"), r))
-
-    def top(r):
-        return max(i for i in range(levels) if (r >> i) & 1)
-
-    def slot_of(r, i):
-        return r * (levels + 1) + i
-
-    def own_sends(s):
-        for i in range(levels):
-            x_copy(s, 0, i).start()
+    order = sorted(range(1, chips), key=lambda m: (bin(m).count("1"), m))
+
+    def later(mask):
+        first = mask.bit_length()
+        return [(mask * levels + i, i) for i in range(first, levels)]
+
+    def own_unit(s, r):
+        if r > 0:
+            zz = sender[r]
+            same(unit_of(s, zz, t), zs.at[s, 0], zr.at[s, zz], here).wait_recv()
+        for slot, i in later(0):
+            x_copy(s, r, t, slot, i).start()
+        if r == Z - 1:
+            f_copy(s, t, 0).start()
+
+    def pass_unit(s, r, level):
+        for mask in order:
+            if bin(mask).count("1") != level:
+                continue
+            src = source(mask)
+            same(unit_of(s, sender[r], src), zs.at[s, 0], xr.at[s, src, sender[r]], here).wait_recv()
+            for slot, i in later(mask):
+                x_copy(s, r, src, slot, i).start()
+            if r == Z - 1:
+                f_copy(s, src, mask).start()
 
     def z_step(s):
-        for d in range(1, Z):
-            zz = (z + d) % Z
-            same(unit_of(s, zz, t), zs.at[s, 0], zr.at[s, zz], here).wait_recv()
-        for d in range(1, Z):
-            for i in range(levels):
-                x_copy(s, d, i).start()
-        f_copy(s, t, slot_of(0, 0), partner).start()
+        for r in range(1, Z):
+            own_unit(s, r)
 
     def f_step(s, level):
-        for r in order:
-            if bin(r).count("1") != level:
-                continue
-            src = source(r)
-            if level == 1:
-                same(unit_of(s, z, src), zs.at[s, 0], xr.at[s, src, 0], here).wait_recv()
-                same(
-                    gat.at[:, s, pl.ds(0, Z - 1), src], zs.at[s, 0], xr.at[s, src, 1], here
-                ).wait_recv()
-            else:
-                same(column(s, src), zs.at[s, 0], fr.at[s, src], here).wait_recv()
-            for i in range(top(r) + 1, levels):
-                f_copy(s, src, slot_of(r, i + 1), flip(chip, bits[i]) * 2 + core).start()
-            f_copy(s, src, slot_of(r, 0), partner).start()
+        for r in range(Z):
+            pass_unit(s, r, level)
 
     def end_step(s):
         for c in range(chips):
@@ -217,24 +225,42 @@
             f_step(s, level)
 
     def drain_gather(s):
-        for d in range(1, Z):
-            z_copy(s, d).wait_send()
-        for d in range(Z):
-            for i in range(levels):
-                x_copy(s, d, i).wait_send()
-        f_copy(s, t, slot_of(0, 0), partner).wait_send()
-        for r in order:
-            src = source(r)
-            for i in range(top(r) + 1, levels):
-                f_copy(s, src, slot_of(r, i + 1), flip(chip, bits[i]) * 2 + core).wait_send()
-            f_copy(s, src, slot_of(r, 0), partner).wait_send()
+        for r in range(1, Z):
+            z_copy(s, r).wait_send()
+        for mask in [0] + order:
+            src = source(mask)
+            for slot, i in later(mask):
+                for r in range(Z):
+                    x_copy(s, r, src, slot, i).wait_send()
+            f_copy(s, src, mask).wait_send()
+
+    def half_copy(kind, s):
+        return remote(
+            part.at[kind, s, :, 1 - core], half_in.at[kind, s], ps.at[kind, s, 0], hr.at[kind, s],
+            {"tp": partner},
+        )
 
     def p_copy(kind, s, d):
-        to = (t + d) % TP
+        to = (chip + d) % chips
         return remote(
-            part.at[kind, s, to], parts_in.at[kind, s, t], ps.at[kind, s, d], pr.at[kind, s],
-            {"tp": to},
+            part.at[kind, s, to, core], parts_in.at[kind, s, chip], ps.at[kind, s, d],
+            pr.at[kind, s], {"tp": to * 2 + core},
         )
+
+    def half_sends(s):
+        for kind in range(2):
+            half_copy(kind, s).start()
+
+    def p_sends(s):
+        for kind in range(2):
+            half_copy(kind, s).wait_recv()
+            for d in range(chips):
+                c = (chip + d) % chips
+                part[kind, s, c, core] = (
+                    part[kind, s, c, core].astype(F32) + half_in[kind, s, c].astype(F32)
+                ).astype(BF)
+            for d in range(1, chips):
+                p_copy(kind, s, d).start()
 
     def out_copies(s):
         return [
@@ -246,13 +272,8 @@
             ))
         ]
 
-    @pl.loop(0, S)
-    def _(s):
-        z_sends(s)
-
-    own_sends(0)
-    if S > 1:
-        own_sends(1)
+    z_sends(0)
+    own_unit(0, 0)
 
     lane = lax.broadcasted_iota(jnp.int32, (L, pair), 1) % HEAD_DIM
     place = lax.broadcasted_iota(jnp.int32, (L, pair), 0).astype(F32)
@@ -268,12 +289,23 @@
     for load in loads:
         load.wait()
 
-    z_step(0)
-    f_step(0, 1)
-    if S > 1:
-        z_step(1)
-    upper_steps(0)
+    for r in range(1, Z + 3):
+        if r < Z:
+            own_unit(0, r)
+        if r == Z // 2 and S > 1:
+            z_sends(1)
+            own_unit(1, 0)
+        if 1 <= r <= Z:
+            pass_unit(0, r - 1, 1)
+        for level in range(2, levels + 1):
+            if 0 <= r - level < Z:
+                pass_unit(0, r - level, level)
     end_step(0)
+
+    @pl.loop(2, S)
+    def _(s):
+        z_sends(s)
+        own_unit(s, 0)
 
     def turned(x, sign):
         return (
@@ -284,27 +316,30 @@
 
     @pl.loop(0, S)
     def _(s):
-        rows_n = gat[0, s].reshape(L, D)
-        rows_g = gat[1, s].reshape(L, D)
+        def rows_n():
+            return gat[0, s].reshape(L, D)
+
+        def rows_g():
+            return gat[1, s].reshape(L, D)
 
         @pl.when(s > 0)
         def _():
             for copy in out_copies(s - 1):
                 copy.wait()
 
-        @pl.when(s + 2 < S)
-        def _():
-            own_sends(s + 2)
-
         @pl.loop(0, 3)
         def _(j):
-            proj[j] = dot(rows_n, wa[j], (1, 0)) + abias_ref[j]
-
-        cgrad[...] = dot(rows_g, wo[...], (1, 1)).astype(BF)
-
-        @pl.when(s + 1 < S)
+            proj[j] = dot(rows_n(), wa[j], (1, 0)) + abias_ref[j]
+
+        cgrad[...] = dot(rows_g(), wo[...], (1, 1)).astype(BF)
+
+        @pl.when((s == 0) & (s + 1 < S))
         def _():
-            f_step(s + 1, 1)
+            z_step(s + 1)
+
+        @pl.when(s > 0)
+        def _():
+            p_sends(s - 1)
 
         @pl.loop(0, local // pair)
         def _(h):
@@ -318,24 +353,36 @@
                 dproj[j, :, lanes] = value.astype(BF)
                 abg_ref[j : j + 1, lanes] += jnp.sum(value, axis=0, keepdims=True)
 
+            @pl.when((h == 0) & (s > 0) & (s + 1 < S))
+            def _():
+                f_step(s + 1, 1)
+
+        tile = min(256, hidden)
+        middle = hidden // tile // 2
+
+        def feed_forward(n):
+            cols = pl.ds(pl.multiple_of(n * tile, tile), tile)
+            value, slope = gelu_parts(dot(rows_n(), wu[:, cols], (1, 0)) + ubias_ref[:, cols])
+            hid[:, cols] = value.astype(BF)
+            grad = dot(rows_g(), wd[cols, :], (1, 1)) * slope
+            pre[:, cols] = grad.astype(BF)
+            ubg_ref[:, cols] += jnp.sum(grad, axis=0, keepdims=True)
+
+        @pl.loop(0, hidden // tile)
+        def _(n):
+            feed_forward(n)
+
+            @pl.when((n == middle) & (s > 0) & (s + 1 < S))
+            def _():
+                upper_steps(s + 1)
+
+            @pl.when((n == middle) & (s == 0) & (s + 1 < S))
+            def _():
+                f_step(s + 1, 1)
+
         @pl.when(s + 2 < S)
         def _():
             z_step(s + 2)
-
-        @pl.when(s + 1 < S)
-        def _():
-            upper_steps(s + 1)
-
-        tile = min(256, hidden)
-
-        @pl.loop(0, hidden // tile)
-        def _(n):
-            cols = pl.ds(pl.multiple_of(n * tile, tile), tile)
-            value, slope = gelu_parts(dot(rows_n, wu[:, cols], (1, 0)) + ubias_ref[:, cols])
-            hid[:, cols] = value.astype(BF)
-            grad = dot(rows_g, wd[cols, :], (1, 1)) * slope
-            pre[:, cols] = grad.astype(BF)
-            ubg_ref[:, cols] += jnp.sum(grad, axis=0, keepdims=True)
 
         for copy in out_copies(s):
             copy.start()
@@ -349,30 +396,31 @@
             back = dot(pre[mine, :], wu[cols, :], (1, 1))
             for j in range(3):
                 back = back + dot(dproj[j, mine, :], wa[j, cols, :], (1, 1))
-            part[0, s, :, :, cols] = out.astype(BF).reshape(TP, R, 256)
-            part[1, s, :, :, cols] = back.astype(BF).reshape(TP, R, 256)
-
-        for kind in range(2):
-            for d in range(1, TP):
-                p_copy(kind, s, d).start()
+            part[0, s, :, :, :, cols] = out.astype(BF).reshape(chips, 2, R, 256)
+            part[1, s, :, :, :, cols] = back.astype(BF).reshape(chips, 2, R, 256)
+
+        half_sends(s)
+
+        @pl.when((s == 0) & (s + 1 < S))
+        def _():
+            upper_steps(s + 1)
 
         @pl.when(s + 1 < S)
         def _():
             end_step(s + 1)
 
+    p_sends(S - 1)
     sum_tp[t] = jnp.zeros_like(sum_tp[t])
 
     @pl.loop(0, S)
     def _(s):
         totals = []
         for kind in range(2):
-            remote(
-                part.at[kind, s, pl.ds(0, TP - 1)], parts_in.at[kind, s, pl.ds(0, TP - 1)],
-                ps.at[kind, s, 0], pr.at[kind, s], here,
-            ).wait_recv()
-            total = part[kind, s, t].astype(F32)
-            for d in range(1, TP):
-                total = total + parts_in[kind, s, (t + d) % TP].astype(F32)
+            incoming = parts_in.at[kind, s, pl.ds(0, chips - 1)]
+            remote(incoming, incoming, ps.at[kind, s, 0], pr.at[kind, s], here).wait_recv()
+            total = part[kind, s, chip, core].astype(F32)
+            for d in range(1, chips):
+                total = total + parts_in[kind, s, (chip + d) % chips].astype(F32)
             totals.append(total)
         branch, ngrad = totals
         x = stream_ref[:, pl.ds(s, 1), :].reshape(R, D)
@@ -390,7 +438,7 @@
             )
         ).reshape(R, 1, D)
         for i, value in enumerate((ngrad * u, ngrad, cot)):
-            sum_tp[t, i : i + 1, :] += jnp.sum(value, axis=0, keepdims=True)
+            sum_tp[t, i] += jnp.sum(value, axis=0, keepdims=True).reshape(D // 128, 128)
 
     def m_copy(d):
         return remote(sum_tp.at[t], sum_tp.at[t], ms.at[d], mr.at[0], {"tp": (t + d) % TP})
@@ -426,7 +474,8 @@
     def _(s):
         drain_gather(s)
         for kind in range(2):
-            for d in range(1, TP):
+            half_copy(kind, s).wait_send()
+            for d in range(1, chips):
                 p_copy(kind, s, d).wait_send()
 
 
@@ -453,7 +502,7 @@
             shape((3, S, L, local), BF),
             shape((R, S, D), F32),
             shape((R, S, D), F32),
-            shape((8, D), F32),
+            shape((3, D // 128, 128), F32),
             shape((3, local), F32),
             shape((1, hidden), F32),
         ],
@@ -472,17 +521,19 @@
             pltpu.VMEM((L, hidden), BF),
             pltpu.VMEM((L, local), BF),
             pltpu.VMEM((3, L, local), BF),
-            pltpu.VMEM((2, S, TP, R, D), BF),
-            pltpu.VMEM((2, S, TP, R, D), BF),
-            pltpu.VMEM((TP, 8, D), F32),
-            pltpu.VMEM((Z, 8, D), F32),
+            pltpu.VMEM((2, S, chips, 2, R, D), BF),
+            pltpu.VMEM((2, S, chips, R, D), BF),
+            pltpu.VMEM((2, S, chips, R, D), BF),
+            pltpu.VMEM((TP, 3, D // 128, 128), F32),
+            pltpu.VMEM((Z, 3, D // 128, 128), F32),
             dma((S, Z)),
             dma((S, Z)),
-            dma((S, levels, Z)),
-            dma((S, TP, 2)),
-            dma((S, chips * (levels + 1))),
+            dma((S, chips * levels, Z)),
+            dma((S, TP, Z)),
+            dma((S, chips)),
             dma((S, TP)),
-            dma((2, S, TP)),
+            dma((2, S, chips)),
+            dma((2, S)),
             dma((2, S)),
             dma((TP + Z,)),
             dma((2,)),
@@ -494,6 +545,78 @@
         ),
         name="block",
     )(stream, cotangent, gain, offset, fbias, abias, ubias, wa, wo, wu, wd)
+
+
+def weight_kernel(steps, normed, grads, pre, dproj, hid_hbm, ctx_hbm, up, attend, down, output, hid, ctx, sem):
+    i = pl.program_id(0)
+    loads = [
+        pltpu.make_async_copy(hid_hbm, hid, sem.at[0]),
+        pltpu.make_async_copy(ctx_hbm, ctx, sem.at[1]),
+    ]
+
+    @pl.when(i == 0)
+    def _():
+        for load in loads:
+            load.start()
+
+    @pl.when(i < steps)
+    def _():
+        up[...] = dot(normed[...], pre[...], (0, 0))
+        for j in range(3):
+            attend[j] = dot(normed[...], dproj[j], (0, 0))
+
+    @pl.when(i == steps)
+    def _():
+        for load in loads:
+            load.wait()
+
+    @pl.when(i >= steps)
+    def _():
+        down[...] = dot(hid[...], grads[...], (0, 0))
+        output[...] = dot(ctx[...], grads[...], (0, 0))
+
+
+def weight_call(normed, grads, pre, dproj, hid, ctx):
+    tokens, D = normed.shape
+    hidden, local = pre.shape[1], ctx.shape[1]
+    tile = 512 if tokens * 512 * 2 <= (2 << 20) else 256
+    steps = D // tile
+    whole = lambda *shape: pl.BlockSpec(shape, lambda i: (0,) * len(shape), pipeline_mode=pl.Buffered(1))
+    first = lambda i: jnp.minimum(i, steps - 1)
+    second = lambda i: jnp.maximum(i - steps, 0)
+    anywhere = pl.BlockSpec(memory_space=pl.ANY)
+    shape = jax.ShapeDtypeStruct
+    return pl.pallas_call(
+        functools.partial(weight_kernel, steps),
+        grid=(2 * steps,),
+        in_specs=[
+            pl.BlockSpec((tokens, tile), lambda i: (0, first(i))),
+            pl.BlockSpec((tokens, tile), lambda i: (0, second(i))),
+            whole(tokens, hidden),
+            whole(3, tokens, local),
+            anywhere,
+            anywhere,
+        ],
+        out_specs=[
+            pl.BlockSpec((tile, hidden), lambda i: (first(i), 0)),
+            pl.BlockSpec((3, tile, local), lambda i: (0, first(i), 0)),
+            pl.BlockSpec((hidden, tile), lambda i: (0, second(i))),
+            pl.BlockSpec((local, tile), lambda i: (0, second(i))),
+        ],
+        out_shape=[
+            shape((D, hidden), F32),
+            shape((3, D, local), F32),
+            shape((hidden, D), F32),
+            shape((local, D), F32),
+        ],
+        scratch_shapes=[
+            pltpu.VMEM((tokens, hidden), BF),
+            pltpu.VMEM((tokens, local), BF),
+            pltpu.SemaphoreType.DMA((2,)),
+        ],
+        compiler_params=pltpu.CompilerParams(vmem_limit_bytes=67000000),
+        name="weights",
+    )(normed, grads, pre, dproj, hid, ctx)
 
 
 def per_device(
@@ -522,26 +645,22 @@
         final_bias.reshape(1, D), attend_bias.reshape(3, 1, local), up_bias.reshape(1, hidden),
         weights, output_weight, up_weight, down_weight, Z, TP,
     )
-    normed = normed.reshape(tokens, D)
-    grads = grads.reshape(tokens, D)
-    output_grad = dot(ctx.reshape(tokens, local), grads, (0, 0))
-    down_grad = dot(hid.reshape(tokens, hidden), grads, (0, 0))
-    up_grad = dot(normed, pre.reshape(tokens, hidden), (0, 0))
-    attend_grad = jnp.swapaxes(
-        jnp.stack([dot(normed, dproj[j].reshape(tokens, local), (0, 0)) for j in range(3)]), 0, 1
+    up_grad, attend_grad, down_grad, output_grad = weight_call(
+        normed.reshape(tokens, D), grads.reshape(tokens, D), pre.reshape(tokens, hidden),
+        dproj.reshape(3, tokens, local), hid.reshape(tokens, hidden), ctx.reshape(tokens, local),
     )
     return (
         result,
         stream_grad,
-        sums[0],
-        sums[1],
-        attend_grad,
+        sums[0].reshape(D),
+        sums[1].reshape(D),
+        jnp.swapaxes(attend_grad, 0, 1),
         abias_grad,
         output_grad,
         up_grad,
         ubias_grad.reshape(hidden),
         down_grad,
-        sums[2],
+        sums[2].reshape(D),
     )
 
 

time: 239 us -> 199 us (0.83)
  matrix products: 40.5 us -> 0 us
  other arithmetic: 3.11 us -> 0 us
    dot_general x6 -> x0, matrix products: 40.5 us -> none  [dot(): lax.dot_general(a, b, ((dims[:1], dims[1:]), ((), ())), preferred_element...]
    pallas_call x0 -> x1, Pallas kernels: none -> 35.5 us  [weight_call(): pl.pallas_call(functools.partial(weight_kernel, steps), grid=(2 * steps,)...]
    pallas_call x1, Pallas kernels: 188 us -> 155 us  [block_call(): pl.pallas_call(functools.partial(block_kernel, (Z, TP, S, R, D)), in_spec...]
    transpose x1 -> x0, other arithmetic: 3.11 us -> none  [per_device(): jnp.swapaxes(jnp.stack([dot(normed, dproj[j].reshape(tokens, local), (0,...]
    unnamed x22 -> x8, local copies, waits for them, and re-layouts: 2.81 us -> 4.96 us
where the time goes in v3:
time: 199 us
  Pallas kernels  190 us (95%)
  local copies, waits for them, and re-layouts  7.57 us (4%)
    pallas_call x1, Pallas kernels, block_call(): pl.pallas_call(functools.partial(block_kernel, (Z, TP, S, R, D)), in_spec...  155 us
    pallas_call x1, Pallas kernels, weight_call(): pl.pallas_call(functools.partial(weight_kernel, steps), grid=(2 * steps,)...  35.5 us
    unnamed x8, local copies, waits for them, and re-layouts  4.96 us

profile of v3, /device:TPU:0, one launch (start us, length us, event | category | flops | bytes accessed | tf_op | source)
XLA Modules:
  0.0 198.5 jit_solution(12784263912271501089)
XLA Ops:
  0.6 1.3 reshape.61.abias_ref
  1.9 154.8 %block.1 = (bf16[4,4,8,16,2048]{4,3,2,1,0:T(8,128)(2,1)}, bf16[4,4,8,16,2048]{4,3,2,1,0:T(8,128)(2,1)}, bf16[4,512,1024]{2,1,0:T(8,128)(2,1)}, bf16[4,512,1024]{...) custom-call(f32[16,4,2048]{2,1,0:T(4,128)} %stream_ref.1, ...), custom_call_target="tpu_custom_call" | custom-call | tf_op jit(solution)/shard_map/block/pallas_call | solution.py:492
  156.7 1.3 slice_bitcast_fusion
  158.0 0.0 copy-start.1
  158.0 0.0 copy-start
  158.0 35.5 %weights.1 = (f32[2048,1024]{1,0:T(8,128)}, f32[3,2048,256]{2,1,0:T(8,128)}, f32[1024,2048]{1,0:T(8,128)}, f32[256,2048]{1,0:T(8,128)}) custom-call(bf16[2048,2048]{1,0:T(8,128)(2,1)} %bitcast.19, bf16[2048,2048]{1,0:T(8,128)(2,1)} %bitcast.20, bf16[2048,1024]{1,0:T(8,128)(2,1)} %bitcast.22, bf16[3,2048,256]{2,1,0:T(8,128)(2,1)} %bitcast.23, ...), custom_call_target="tpu_custom_call" | custom-call | tf_op jit(solution)/shard_map/weights/pallas_call | solution.py:589
  193.6 1.9 copy.26
  195.5 1.9 copy.27
  197.3 0.0 copy-done.1
  197.3 0.6 copy.28
  197.9 0.0 copy-done
  197.9 0.6 copy.29
Async XLA Ops:
  158.0 39.3 %copy-start.1 = (f32[3,256]{1,0:T(4,128)S(1)}, f32[3,256]{1,0:T(4,128)}, u32[]{:S(2)}) copy-start(f32[3,256]{1,0:T(4,128)} %get-tuple-element.60) | copy-start | bytes 9220
  158.0 39.9 %copy-start = (f32[1,1024]{1,0:T(1,128)S(1)}, f32[1,1024]{1,0:T(1,128)}, u32[]{:S(2)}) copy-start(f32[1,1024]{1,0:T(1,128)} %get-tuple-element.39) | copy-start | bytes 12292

commit v4 on v3

--- a/solution.py
+++ b/solution.py
@@ -47,45 +47,72 @@
     return index
 
 
-def head_pass(q_all, k_all, v_all, g_all, heads):
-    length = q_all.shape[0]
-    scale = HEAD_DIM ** (-0.5)
-    block = min(256, length)
-    results = ([], [], [], [])
-    for head in range(heads):
-        lanes = slice(head * HEAD_DIM, (head + 1) * HEAD_DIM)
-        q, k, v, g = q_all[:, lanes], k_all[:, lanes], v_all[:, lanes], g_all[:, lanes]
-        ctx_rows, dq_rows = [], []
-        dk = dv = None
-        for start in range(0, length, block):
-            stop = start + block
-            qb, gb = q[start:stop], g[start:stop]
-            s = dot(qb, k[:stop], (1, 1)) * scale
-            row = lax.broadcasted_iota(jnp.int32, s.shape, 0) + start
-            col = lax.broadcasted_iota(jnp.int32, s.shape, 1)
-            s = jnp.where(row >= col, s, -jnp.inf)
-            m = jnp.max(s, axis=1, keepdims=True)
-            p = jnp.exp(s - m)
-            p = p * (1.0 / jnp.sum(p, axis=1, keepdims=True))
-            pb = p.astype(BF)
-            ctx = dot(pb, v[:stop], (1, 0)).astype(BF)
-            delta = jnp.sum(gb.astype(F32) * ctx.astype(F32), axis=1, keepdims=True)
-            dp = dot(gb, v[:stop], (1, 1))
-            ds = (p * (dp - delta) * scale).astype(BF)
-            ctx_rows.append(ctx)
-            dq_rows.append(dot(ds, k[:stop], (1, 0)))
-            dvb = dot(pb, gb, (0, 0))
-            dkb = dot(ds, qb, (0, 0))
-            if start == 0:
-                dk, dv = dkb, dvb
+def head_pass(q_all, k_all, v_all, g_all, heads, block=256):
+    length, width = q_all.shape
+    scale = jnp.asarray(HEAD_DIM ** (-0.5), BF)
+    block = min(block, length)
+    lane = lax.broadcasted_iota(jnp.int32, (1, width), 1) // HEAD_DIM
+    zero = jnp.zeros((), BF)
+    parts = [(start, head) for start in range(0, length, block) for head in range(heads)]
+
+    def masked(x, start, head):
+        return jnp.where(lane == head, x[start : start + block], zero)
+
+    qs = [masked(q_all, a, h) * scale for a, h in parts]
+    gs = [masked(g_all, a, h) for a, h in parts]
+
+    def weights(s, start):
+        diag = s[:, start:]
+        row = lax.broadcasted_iota(jnp.int32, diag.shape, 0)
+        col = lax.broadcasted_iota(jnp.int32, diag.shape, 1)
+        diag = jnp.where(row >= col, diag, -jnp.inf)
+        s = diag if start == 0 else jnp.concatenate([s[:, :start], diag], axis=1)
+        p = jnp.exp(s - jnp.max(s, axis=1, keepdims=True))
+        return p * (1.0 / jnp.sum(p, axis=1, keepdims=True))
+
+    cs, dqs, dks, dvs = [], [], [], []
+    together = len(parts) if length <= 512 else heads
+    for first in range(0, len(parts), together):
+        group = slice(first, first + together)
+        stops = [a + block for a, h in parts[group]]
+        gq, gg = qs[group], gs[group]
+        ss = [dot(q, k_all[:n], (1, 1)) for q, n in zip(gq, stops)]
+        dps = [dot(g, v_all[:n], (1, 1)) for g, n in zip(gg, stops)]
+        ps = [weights(s, a) for s, (a, h) in zip(ss, parts[group])]
+        pbs = [p.astype(BF) for p in ps]
+        gc = [dot(p, v_all[:n], (1, 0)).astype(BF) for p, n in zip(pbs, stops)]
+        dvs += [dot(g, p, (0, 0)) for g, p in zip(gg, pbs)]
+        deltas = [
+            jnp.sum(g.astype(F32) * c.astype(F32), axis=1, keepdims=True) for g, c in zip(gg, gc)
+        ]
+        dss = [(p * (dp - delta)).astype(BF) for p, dp, delta in zip(ps, dps, deltas)]
+        dqs += [dot(ds, k_all[:n], (1, 0)) for ds, n in zip(dss, stops)]
+        dks += [dot(q, ds, (0, 0)) for q, ds in zip(gq, dss)]
+        cs += gc
+
+    def rows(values):
+        blocks = []
+        for n in range(0, len(parts), heads):
+            value = values[n]
+            for h in range(1, heads):
+                value = jnp.where(lane == h, values[n + h], value)
+            blocks.append(value)
+        return jnp.concatenate(blocks, axis=0)
+
+    def columns(values):
+        total = None
+        for n in range(0, len(parts), heads):
+            value = values[n]
+            for h in range(1, heads):
+                value = value + values[n + h]
+            if total is None:
+                total = value
             else:
-                dk = jnp.concatenate([dk + dkb[:start], dkb[start:]], axis=0)
-                dv = jnp.concatenate([dv + dvb[:start], dvb[start:]], axis=0)
-        results[0].append(jnp.concatenate(ctx_rows, axis=0))
-        results[1].append(jnp.concatenate(dq_rows, axis=0))
-        results[2].append(dk)
-        results[3].append(dv)
-    return [jnp.concatenate(parts, axis=1) for parts in results]
+                old = total.shape[1]
+                total = jnp.concatenate([total + value[:, :old], value[:, old:]], axis=1)
+        return total.T
+
+    return [rows(cs), rows(dqs) * scale.astype(F32), columns(dks), columns(dvs)]
 
 
 def block_kernel(
@@ -93,9 +120,9 @@
     stream_ref, cot_ref, gain_ref, offset_ref, fbias_ref, abias_ref, ubias_ref,
     wa_hbm, wo_hbm, wu_hbm, wd_hbm,
     norm_out, grad_out, hid_out, pre_out, ctx_out, dproj_out,
-    result_ref, sgrad_ref, sums_ref, abg_ref, ubg_ref,
+    result_ref, sgrad_ref, gsum_ref, osum_ref, fsum_ref, abg_ref, ubg_ref,
     gat, wa, wo, wu, wd, unit, istd, table, proj, cgrad, hid, pre, ctx, dproj,
-    part, half_in, parts_in, sum_tp, sum_seq,
+    part, half_in, parts_in, sum_tp, sum_seq, ubg,
     zs, zr, xs, xr, fs, fr, ps, hr, pr, ms, mr, ws, os,
 ):
     Z, TP, S, R, D = dims
@@ -125,8 +152,7 @@
     for d in range(1, Z):
         pl.semaphore_signal(barrier, inc=1, device_id={"seq": (z + d) % Z}, device_id_type=MESH)
 
-    @pl.loop(0, S)
-    def _(s):
+    def normalize(s):
         x = stream_ref[:, pl.ds(s, 1), :].reshape(R, D)
         mean = jnp.mean(x, axis=-1, keepdims=True)
         centred = x - mean
@@ -137,6 +163,7 @@
         gat[0, s, z, t] = (u * gain_ref[...] + offset_ref[...]).astype(BF)
         gat[1, s, z, t] = cot_ref[:, pl.ds(s, 1), :].reshape(R, D).astype(BF)
 
+    normalize(0)
     pl.semaphore_wait(barrier, TP + Z - 2)
 
     def remote(src, dst, ssem, rsem, dev):
@@ -207,22 +234,10 @@
             if r == Z - 1:
                 f_copy(s, src, mask).start()
 
-    def z_step(s):
-        for r in range(1, Z):
-            own_unit(s, r)
-
-    def f_step(s, level):
-        for r in range(Z):
-            pass_unit(s, r, level)
-
     def end_step(s):
         for c in range(chips):
             src = ((chip + c) % chips) * 2 + 1 - core
             same(column(s, src), zs.at[s, 0], fr.at[s, src], here).wait_recv()
-
-    def upper_steps(s):
-        for level in range(2, levels + 1):
-            f_step(s, level)
 
     def drain_gather(s):
         for r in range(1, Z):
@@ -272,8 +287,34 @@
             ))
         ]
 
+    def group_steps(n):
+        steps = []
+        if n % Z == 1:
+            steps.append((n // Z + 1, z_sends))
+        for level in range(levels + 1):
+            m = n - 2 * level
+            if m > 0 and level == 0:
+                steps.append((m // Z, functools.partial(own_unit, r=m % Z)))
+            elif m >= 0 and level > 0:
+                steps.append((m // Z, functools.partial(pass_unit, r=m % Z, level=level)))
+        return steps
+
+    lead = 2 * levels
+
+    def run_groups(s, part):
+        for k in range(Z * part // 4, Z * (part + 1) // 4):
+            for i, step in group_steps(Z + lead + k):
+
+                @pl.when(s + i < S)
+                def _(step=step, i=i):
+                    step(s + i)
+
     z_sends(0)
     own_unit(0, 0)
+
+    @pl.loop(1, S)
+    def _(s):
+        normalize(s)
 
     lane = lax.broadcasted_iota(jnp.int32, (L, pair), 1) % HEAD_DIM
     place = lax.broadcasted_iota(jnp.int32, (L, pair), 0).astype(F32)
@@ -282,37 +323,22 @@
     angle = place * freq
     cosine, sine = jnp.cos(angle), jnp.sin(angle)
     table[0] = jnp.where(lane < ROT, cosine, 1.0)
-    table[1] = jnp.where(lane < half, -sine, 0.0)
-    table[2] = jnp.where((lane >= half) & (lane < ROT), sine, 0.0)
+    table[1] = jnp.where(lane < half, -sine, jnp.where(lane < ROT, sine, 0.0))
     abg_ref[...] = jnp.zeros_like(abg_ref)
-    ubg_ref[...] = jnp.zeros_like(ubg_ref)
+    ubg[...] = jnp.zeros_like(ubg)
     for load in loads:
         load.wait()
 
-    for r in range(1, Z + 3):
-        if r < Z:
-            own_unit(0, r)
-        if r == Z // 2 and S > 1:
-            z_sends(1)
-            own_unit(1, 0)
-        if 1 <= r <= Z:
-            pass_unit(0, r - 1, 1)
-        for level in range(2, levels + 1):
-            if 0 <= r - level < Z:
-                pass_unit(0, r - level, level)
+    for n in range(1, Z + lead):
+        for i, step in group_steps(n):
+            if i < S:
+                step(i)
     end_step(0)
 
-    @pl.loop(2, S)
-    def _(s):
-        z_sends(s)
-        own_unit(s, 0)
-
     def turned(x, sign):
-        return (
-            x * table[0]
-            + sign * pltpu.roll(x, pair - half, 1) * table[1]
-            + sign * pltpu.roll(x, half, 1) * table[2]
-        )
+        first = lax.broadcasted_iota(jnp.int32, (1, pair), 1) % HEAD_DIM < half
+        crossed = jnp.where(first, pltpu.roll(x, pair - half, 1), pltpu.roll(x, half, 1))
+        return x * table[0] + sign * (crossed * table[1])
 
     @pl.loop(0, S)
     def _(s):
@@ -329,13 +355,9 @@
 
         @pl.loop(0, 3)
         def _(j):
-            proj[j] = dot(rows_n(), wa[j], (1, 0)) + abias_ref[j]
+            proj[j] = dot(rows_n(), wa[j], (1, 0)) + abias_ref[pl.ds(j, 1), :]
 
         cgrad[...] = dot(rows_g(), wo[...], (1, 1)).astype(BF)
-
-        @pl.when((s == 0) & (s + 1 < S))
-        def _():
-            z_step(s + 1)
 
         @pl.when(s > 0)
         def _():
@@ -353,11 +375,11 @@
                 dproj[j, :, lanes] = value.astype(BF)
                 abg_ref[j : j + 1, lanes] += jnp.sum(value, axis=0, keepdims=True)
 
-            @pl.when((h == 0) & (s > 0) & (s + 1 < S))
+            @pl.when(h == 0)
             def _():
-                f_step(s + 1, 1)
-
-        tile = min(256, hidden)
+                run_groups(s, 0)
+
+        tile = 256 if L <= 512 else 128
         middle = hidden // tile // 2
 
         def feed_forward(n):
@@ -366,23 +388,19 @@
             hid[:, cols] = value.astype(BF)
             grad = dot(rows_g(), wd[cols, :], (1, 1)) * slope
             pre[:, cols] = grad.astype(BF)
-            ubg_ref[:, cols] += jnp.sum(grad, axis=0, keepdims=True)
+            ubg[:, cols] += jnp.sum(grad, axis=0, keepdims=True)
 
         @pl.loop(0, hidden // tile)
         def _(n):
             feed_forward(n)
 
-            @pl.when((n == middle) & (s > 0) & (s + 1 < S))
+            @pl.when(n == 0)
             def _():
-                upper_steps(s + 1)
-
-            @pl.when((n == middle) & (s == 0) & (s + 1 < S))
+                run_groups(s, 1)
+
+            @pl.when(n == middle)
             def _():
-                f_step(s + 1, 1)
-
-        @pl.when(s + 2 < S)
-        def _():
-            z_step(s + 2)
+                run_groups(s, 2)
 
         for copy in out_copies(s):
             copy.start()
@@ -401,9 +419,7 @@
 
         half_sends(s)
 
-        @pl.when((s == 0) & (s + 1 < S))
-        def _():
-            upper_steps(s + 1)
+        run_groups(s, 3)
 
         @pl.when(s + 1 < S)
         def _():
@@ -461,7 +477,8 @@
     total = sum_seq[0]
     for d in range(1, Z):
         total = total + sum_seq[d]
-    sums_ref[...] = total
+    gsum_ref[...], osum_ref[...], fsum_ref[...] = total[0], total[1], total[2]
+    ubg_ref[...] = ubg[...].reshape(hidden // 128, 128)
 
     for d in range(1, TP):
         m_copy(d).wait_send()
@@ -492,7 +509,7 @@
     return pl.pallas_call(
         functools.partial(block_kernel, (Z, TP, S, R, D)),
         in_specs=[vm] * 7 + [anywhere] * 4,
-        out_specs=[anywhere] * 6 + [vm] * 5,
+        out_specs=[anywhere] * 6 + [vm] * 7,
         out_shape=[
             shape((S, Z, TP, R, D), BF),
             shape((S, Z, TP, R, D), BF),
@@ -502,9 +519,11 @@
             shape((3, S, L, local), BF),
             shape((R, S, D), F32),
             shape((R, S, D), F32),
-            shape((3, D // 128, 128), F32),
+            shape((D // 128, 128), F32),
+            shape((D // 128, 128), F32),
+            shape((D // 128, 128), F32),
             shape((3, local), F32),
-            shape((1, hidden), F32),
+            shape((hidden // 128, 128), F32),
         ],
         scratch_shapes=[
             pltpu.VMEM((2, S, Z, TP, R, D), BF),
@@ -514,7 +533,7 @@
             pltpu.VMEM((hidden, D), BF),
             pltpu.VMEM((S, R, D), F32),
             pltpu.VMEM((S, R, 128), F32),
-            pltpu.VMEM((3, L, min(128, local)), F32),
+            pltpu.VMEM((2, L, min(128, local)), F32),
             pltpu.VMEM((3, L, local), F32),
             pltpu.VMEM((L, local), BF),
             pltpu.VMEM((L, hidden), BF),
@@ -526,6 +545,7 @@
             pltpu.VMEM((2, S, chips, R, D), BF),
             pltpu.VMEM((TP, 3, D // 128, 128), F32),
             pltpu.VMEM((Z, 3, D // 128, 128), F32),
+            pltpu.VMEM((1, hidden), F32),
             dma((S, Z)),
             dma((S, Z)),
             dma((S, chips * levels, Z)),
@@ -547,7 +567,11 @@
     )(stream, cotangent, gain, offset, fbias, abias, ubias, wa, wo, wu, wd)
 
 
-def weight_kernel(steps, normed, grads, pre, dproj, hid_hbm, ctx_hbm, up, attend, down, output, hid, ctx, sem):
+def weight_kernel(steps, normed, grads, pre, dproj, hid_hbm, ctx_hbm, *rest):
+    smalls = (len(rest) - 7) // 2
+    given, rest = rest[:smalls], rest[smalls:]
+    up, attend, down, output = rest[:4]
+    handed, (hid, ctx, sem) = rest[4 : 4 + smalls], rest[4 + smalls :]
     i = pl.program_id(0)
     loads = [
         pltpu.make_async_copy(hid_hbm, hid, sem.at[0]),
@@ -558,6 +582,8 @@
     def _():
         for load in loads:
             load.start()
+        for source, target in zip(given, handed):
+            target[...] = source[...]
 
     @pl.when(i < steps)
     def _():
@@ -576,7 +602,7 @@
         output[...] = dot(ctx[...], grads[...], (0, 0))
 
 
-def weight_call(normed, grads, pre, dproj, hid, ctx):
+def weight_call(normed, grads, pre, dproj, hid, ctx, smalls):
     tokens, D = normed.shape
     hidden, local = pre.shape[1], ctx.shape[1]
     tile = 512 if tokens * 512 * 2 <= (2 << 20) else 256
@@ -596,19 +622,22 @@
             whole(3, tokens, local),
             anywhere,
             anywhere,
-        ],
+        ]
+        + [whole(*small.shape) for small in smalls],
         out_specs=[
             pl.BlockSpec((tile, hidden), lambda i: (first(i), 0)),
             pl.BlockSpec((3, tile, local), lambda i: (0, first(i), 0)),
             pl.BlockSpec((hidden, tile), lambda i: (0, second(i))),
             pl.BlockSpec((local, tile), lambda i: (0, second(i))),
-        ],
+        ]
+        + [whole(*small.shape) for small in smalls],
         out_shape=[
             shape((D, hidden), F32),
             shape((3, D, local), F32),
             shape((hidden, D), F32),
             shape((local, D), F32),
-        ],
+        ]
+        + [shape(small.shape, F32) for small in smalls],
         scratch_shapes=[
             pltpu.VMEM((tokens, hidden), BF),
             pltpu.VMEM((tokens, local), BF),
@@ -616,7 +645,7 @@
         ],
         compiler_params=pltpu.CompilerParams(vmem_limit_bytes=67000000),
         name="weights",
-    )(normed, grads, pre, dproj, hid, ctx)
+    )(normed, grads, pre, dproj, hid, ctx, *smalls)
 
 
 def per_device(
@@ -639,28 +668,32 @@
     tokens = R * S * TP * Z
     weights = jnp.swapaxes(attend_weight, 0, 1)
     (
-        normed, grads, hid, pre, ctx, dproj, result, stream_grad, sums, abias_grad, ubias_grad
+        normed, grads, hid, pre, ctx, dproj, *smalls
     ) = block_call(
         stream, cotangent, norm_gain.reshape(1, D), norm_offset.reshape(1, D),
-        final_bias.reshape(1, D), attend_bias.reshape(3, 1, local), up_bias.reshape(1, hidden),
+        final_bias.reshape(1, D), attend_bias, up_bias.reshape(1, hidden),
         weights, output_weight, up_weight, down_weight, Z, TP,
     )
-    up_grad, attend_grad, down_grad, output_grad = weight_call(
+    (
+        up_grad, attend_grad, down_grad, output_grad,
+        result, stream_grad, gain_grad, offset_grad, fbias_grad, abias_grad, ubias_grad,
+    ) = weight_call(
         normed.reshape(tokens, D), grads.reshape(tokens, D), pre.reshape(tokens, hidden),
         dproj.reshape(3, tokens, local), hid.reshape(tokens, hidden), ctx.reshape(tokens, local),
+        smalls,
     )
     return (
         result,
         stream_grad,
-        sums[0].reshape(D),
-        sums[1].reshape(D),
+        gain_grad.reshape(D),
+        offset_grad.reshape(D),
         jnp.swapaxes(attend_grad, 0, 1),
         abias_grad,
         output_grad,
         up_grad,
         ubias_grad.reshape(hidden),
         down_grad,
-        sums[2].reshape(D),
+        fbias_grad.reshape(D),
     )
 
 

time: 199 us -> 181 us (0.910)
  Pallas kernels: 190 us -> 180 us
  local copies, waits for them, and re-layouts: 7.57 us -> 0 us
    pallas_call x1, Pallas kernels: 155 us -> 144 us  [block_call(): pl.pallas_call(functools.partial(block_kernel, (Z, TP, S, R, D)), in_spec...]
    unnamed x8 -> x0, local copies, waits for them, and re-layouts: 4.96 us -> none
where the time goes in v4:
time: 181 us
  Pallas kernels  180 us (99%)
    pallas_call x1, Pallas kernels, block_call(): pl.pallas_call(functools.partial(block_kernel, (Z, TP, S, R, D)), in_spec...  144 us
    pallas_call x1, Pallas kernels, weight_call(): pl.pallas_call(functools.partial(weight_kernel, steps), grid=(2 * steps,)...  36.5 us

profile of v4, /device:TPU:0, one launch (start us, length us, event | category | flops | bytes accessed | tf_op | source)
XLA Modules:
  0.0 181.1 jit_solution(15629622793119276371)
XLA Ops:
  0.6 143.8 %block.1 = (bf16[4,4,8,16,2048]{4,3,2,1,0:T(8,128)(2,1)}, bf16[4,4,8,16,2048]{4,3,2,1,0:T(8,128)(2,1)}, bf16[4,512,1024]{2,1,0:T(8,128)(2,1)}, bf16[4,512,1024]{...) custom-call(f32[16,4,2048]{2,1,0:T(4,128)} %stream_ref.1, ...), custom_call_target="tpu_custom_call" | custom-call | tf_op jit(solution)/shard_map/block/pallas_call | solution.py:509
  144.5 36.5 %weights.1 = (f32[2048,1024]{1,0:T(8,128)}, f32[3,2048,256]{2,1,0:T(8,128)}, f32[1024,2048]{1,0:T(8,128)}, f32[256,2048]{1,0:T(8,128)}, f32[16,4,2048]{2,1,0:T(4...) custom-call(bf16[2048,2048]{1,0:T(8,128)(2,1)} %bitcast.16, ...), custom_call_target="tpu_custom_call" | custom-call | tf_op jit(solution)/shard_map/weights/pallas_call | solution.py:615

commit v5 on v4

--- a/solution.py
+++ b/solution.py
@@ -119,11 +119,11 @@
     dims,
     stream_ref, cot_ref, gain_ref, offset_ref, fbias_ref, abias_ref, ubias_ref,
     wa_hbm, wo_hbm, wu_hbm, wd_hbm,
-    norm_out, grad_out, hid_out, pre_out, ctx_out, dproj_out,
+    norm_out, grad_out, hid_out, pre_out, wide_out, tall_out,
     result_ref, sgrad_ref, gsum_ref, osum_ref, fsum_ref, abg_ref, ubg_ref,
     gat, wa, wo, wu, wd, unit, istd, table, proj, cgrad, hid, pre, ctx, dproj,
-    part, half_in, parts_in, sum_tp, sum_seq, ubg,
-    zs, zr, xs, xr, fs, fr, ps, hr, pr, ms, mr, ws, os,
+    part, half_in, parts_in, sum_tp, sum_seq, ubg, wide, tall,
+    zs, zr, xs, xr, fs, fr, ps, hr, pr, ms, mr, ws, os, gs,
 ):
     Z, TP, S, R, D = dims
     z, t = lax.axis_index("seq"), lax.axis_index("tp")
@@ -139,6 +139,7 @@
     hidden = wu.shape[1]
     pair = min(128, local)
     own_rows = TP * R
+    inside = ctx.shape[0] == S
 
     loads = [
         pltpu.make_async_copy(src, dst, ws.at[i])
@@ -278,14 +279,13 @@
                 p_copy(kind, s, d).start()
 
     def out_copies(s):
-        return [
-            pltpu.make_async_copy(src, dst, os.at[i])
-            for i, (src, dst) in enumerate((
-                (gat.at[0, s], norm_out.at[s]), (gat.at[1, s], grad_out.at[s]),
-                (hid, hid_out.at[s]), (pre, pre_out.at[s]), (ctx, ctx_out.at[s]),
-                (dproj, dproj_out.at[:, s]),
-            ))
+        pairs = [
+            (gat.at[0, s], norm_out.at[s]), (gat.at[1, s], grad_out.at[s]),
+            (hid, hid_out.at[s]), (pre, pre_out.at[s]),
         ]
+        if not inside:
+            pairs += [(ctx.at[0], tall_out.at[s]), (dproj.at[:, 0], wide_out.at[:, s])]
+        return [pltpu.make_async_copy(src, dst, os.at[i]) for i, (src, dst) in enumerate(pairs)]
 
     def group_steps(n):
         steps = []
@@ -342,6 +342,8 @@
 
     @pl.loop(0, S)
     def _(s):
+        kept = s if inside else 0
+
         def rows_n():
             return gat[0, s].reshape(L, D)
 
@@ -370,9 +372,9 @@
             k = turned(proj[1, :, lanes], 1.0).astype(BF)
             v = proj[2, :, lanes].astype(BF)
             c, dq, dk, dv = head_pass(q, k, v, cgrad[:, lanes], pair // HEAD_DIM)
-            ctx[:, lanes] = c
+            ctx[kept, :, lanes] = c
             for j, value in enumerate((turned(dq, -1.0), turned(dk, -1.0), dv)):
-                dproj[j, :, lanes] = value.astype(BF)
+                dproj[j, kept, :, lanes] = value.astype(BF)
                 abg_ref[j : j + 1, lanes] += jnp.sum(value, axis=0, keepdims=True)
 
             @pl.when(h == 0)
@@ -410,10 +412,10 @@
         @pl.loop(0, D // 256)
         def _(n):
             cols = pl.ds(pl.multiple_of(n * 256, 256), 256)
-            out = dot(ctx[mine, :], wo[:, cols], (1, 0)) + dot(hid[mine, :], wd[:, cols], (1, 0))
+            out = dot(ctx[kept, mine, :], wo[:, cols], (1, 0)) + dot(hid[mine, :], wd[:, cols], (1, 0))
             back = dot(pre[mine, :], wu[cols, :], (1, 1))
             for j in range(3):
-                back = back + dot(dproj[j, mine, :], wa[j, cols, :], (1, 1))
+                back = back + dot(dproj[j, kept, mine, :], wa[j, cols, :], (1, 1))
             part[0, s, :, :, :, cols] = out.astype(BF).reshape(chips, 2, R, 256)
             part[1, s, :, :, :, cols] = back.astype(BF).reshape(chips, 2, R, 256)
 
@@ -425,7 +427,44 @@
         def _():
             end_step(s + 1)
 
+    strip = D // 4
+
+    def strip_of(n):
+        return pl.ds(pl.multiple_of(n * strip, strip), strip)
+
+    def tall_copy():
+        return pltpu.make_async_copy(tall, tall_out, gs.at[2])
+
+    def wide_copy(n, slot):
+        return pltpu.make_async_copy(wide.at[slot], wide_out.at[:, strip_of(n), :], gs.at[slot])
+
+    def output_grads():
+        if inside:
+
+            @pl.loop(0, 4)
+            def _(n):
+                rows = gat[1, :, :, :, :, strip_of(n)].reshape(S * L, strip)
+                tall[:, strip_of(n)] = dot(ctx[...].reshape(S * L, local), rows, (0, 0))
+
+            tall_copy().start()
+
+    def attend_grads(n, slot):
+        if inside:
+
+            @pl.loop(0, 3)
+            def _(j):
+                rows = gat[0, :, :, :, :, strip_of(n)].reshape(S * L, strip)
+                wide[slot, j] = dot(rows, dproj[j].reshape(S * L, local), (0, 0))
+
+            wide_copy(n, slot).start()
+
+    output_grads()
     p_sends(S - 1)
+
+    @pl.loop(0, 2)
+    def _(n):
+        attend_grads(n, n)
+
     sum_tp[t] = jnp.zeros_like(sum_tp[t])
 
     @pl.loop(0, S)
@@ -466,6 +505,9 @@
 
     for d in range(1, TP):
         m_copy(d).start()
+    if inside:
+        wide_copy(0, 0).wait()
+    attend_grads(2, 0)
     same(sum_tp.at[pl.ds(0, TP - 1)], ms.at[0], mr.at[0], here).wait_recv()
     total = sum_tp[0]
     for d in range(1, TP):
@@ -473,6 +515,9 @@
     sum_seq[z] = total
     for d in range(1, Z):
         n_copy(d).start()
+    if inside:
+        wide_copy(1, 1).wait()
+    attend_grads(3, 1)
     same(sum_seq.at[pl.ds(0, Z - 1)], ms.at[0], mr.at[1], here).wait_recv()
     total = sum_seq[0]
     for d in range(1, Z):
@@ -486,6 +531,10 @@
         n_copy(d).wait_send()
     for copy in out_copies(S - 1):
         copy.wait()
+    if inside:
+        tall_copy().wait()
+        wide_copy(2, 0).wait()
+        wide_copy(3, 1).wait()
 
     @pl.loop(0, S)
     def _(s):
@@ -494,6 +543,10 @@
             half_copy(kind, s).wait_send()
             for d in range(1, chips):
                 p_copy(kind, s, d).wait_send()
+
+
+def attention_inside(length):
+    return length <= 512
 
 
 def block_call(stream, cotangent, gain, offset, fbias, abias, ubias, wa, wo, wu, wd, Z, TP):
@@ -506,6 +559,8 @@
     anywhere = pl.BlockSpec(memory_space=pl.ANY)
     shape = jax.ShapeDtypeStruct
     dma = pltpu.SemaphoreType.DMA
+    inside = attention_inside(L)
+    kept = S if inside else 1
     return pl.pallas_call(
         functools.partial(block_kernel, (Z, TP, S, R, D)),
         in_specs=[vm] * 7 + [anywhere] * 4,
@@ -515,8 +570,8 @@
             shape((S, Z, TP, R, D), BF),
             shape((S, L, hidden), BF),
             shape((S, L, hidden), BF),
-            shape((S, L, local), BF),
-            shape((3, S, L, local), BF),
+            shape((3, D, local), F32) if inside else shape((3, S, L, local), BF),
+            shape((local, D), F32) if inside else shape((S, L, local), BF),
             shape((R, S, D), F32),
             shape((R, S, D), F32),
             shape((D // 128, 128), F32),
@@ -538,14 +593,16 @@
             pltpu.VMEM((L, local), BF),
             pltpu.VMEM((L, hidden), BF),
             pltpu.VMEM((L, hidden), BF),
-            pltpu.VMEM((L, local), BF),
-            pltpu.VMEM((3, L, local), BF),
+            pltpu.VMEM((kept, L, local), BF),
+            pltpu.VMEM((3, kept, L, local), BF),
             pltpu.VMEM((2, S, chips, 2, R, D), BF),
             pltpu.VMEM((2, S, chips, R, D), BF),
             pltpu.VMEM((2, S, chips, R, D), BF),
             pltpu.VMEM((TP, 3, D // 128, 128), F32),
             pltpu.VMEM((Z, 3, D // 128, 128), F32),
             pltpu.VMEM((1, hidden), F32),
+            pltpu.VMEM((2, 3, D // 4, local) if inside else (1, 3, 8, 128), F32),
+            pltpu.VMEM((local, D) if inside else (8, 128), F32),
             dma((S, Z)),
             dma((S, Z)),
             dma((S, chips * levels, Z)),
@@ -559,6 +616,7 @@
             dma((2,)),
             dma((4,)),
             dma((6,)),
+            dma((3,)),
         ],
         compiler_params=pltpu.CompilerParams(
             collective_id=0, has_side_effects=True, vmem_limit_bytes=67000000
@@ -567,7 +625,7 @@
     )(stream, cotangent, gain, offset, fbias, abias, ubias, wa, wo, wu, wd)
 
 
-def weight_kernel(steps, normed, grads, pre, dproj, hid_hbm, ctx_hbm, *rest):
+def weight_kernel(steps, inside, normed, grads, pre, wide, hid_hbm, tall, *rest):
     smalls = (len(rest) - 7) // 2
     given, rest = rest[:smalls], rest[smalls:]
     up, attend, down, output = rest[:4]
@@ -575,8 +633,9 @@
     i = pl.program_id(0)
     loads = [
         pltpu.make_async_copy(hid_hbm, hid, sem.at[0]),
-        pltpu.make_async_copy(ctx_hbm, ctx, sem.at[1]),
     ]
+    if not inside:
+        loads.append(pltpu.make_async_copy(tall, ctx, sem.at[1]))
 
     @pl.when(i == 0)
     def _():
@@ -588,8 +647,11 @@
     @pl.when(i < steps)
     def _():
         up[...] = dot(normed[...], pre[...], (0, 0))
-        for j in range(3):
-            attend[j] = dot(normed[...], dproj[j], (0, 0))
+        if inside:
+            attend[...] = wide[...]
+        else:
+            for j in range(3):
+                attend[j] = dot(normed[...], wide[j], (0, 0))
 
     @pl.when(i == steps)
     def _():
@@ -599,12 +661,12 @@
     @pl.when(i >= steps)
     def _():
         down[...] = dot(hid[...], grads[...], (0, 0))
-        output[...] = dot(ctx[...], grads[...], (0, 0))
-
-
-def weight_call(normed, grads, pre, dproj, hid, ctx, smalls):
+        output[...] = tall[...] if inside else dot(ctx[...], grads[...], (0, 0))
+
+
+def weight_call(normed, grads, pre, wide, hid, tall, smalls, local, inside):
     tokens, D = normed.shape
-    hidden, local = pre.shape[1], ctx.shape[1]
+    hidden = pre.shape[1]
     tile = 512 if tokens * 512 * 2 <= (2 << 20) else 256
     steps = D // tile
     whole = lambda *shape: pl.BlockSpec(shape, lambda i: (0,) * len(shape), pipeline_mode=pl.Buffered(1))
@@ -613,15 +675,15 @@
     anywhere = pl.BlockSpec(memory_space=pl.ANY)
     shape = jax.ShapeDtypeStruct
     return pl.pallas_call(
-        functools.partial(weight_kernel, steps),
+        functools.partial(weight_kernel, steps, inside),
         grid=(2 * steps,),
         in_specs=[
             pl.BlockSpec((tokens, tile), lambda i: (0, first(i))),
             pl.BlockSpec((tokens, tile), lambda i: (0, second(i))),
             whole(tokens, hidden),
-            whole(3, tokens, local),
+            pl.BlockSpec((3, tile, local), lambda i: (0, first(i), 0)) if inside else whole(*wide.shape),
             anywhere,
-            anywhere,
+            pl.BlockSpec((local, tile), lambda i: (0, second(i))) if inside else anywhere,
         ]
         + [whole(*small.shape) for small in smalls],
         out_specs=[
@@ -640,12 +702,12 @@
         + [shape(small.shape, F32) for small in smalls],
         scratch_shapes=[
             pltpu.VMEM((tokens, hidden), BF),
-            pltpu.VMEM((tokens, local), BF),
+            pltpu.VMEM((16, 128) if inside else (tokens, local), BF),
             pltpu.SemaphoreType.DMA((2,)),
         ],
         compiler_params=pltpu.CompilerParams(vmem_limit_bytes=67000000),
         name="weights",
-    )(normed, grads, pre, dproj, hid, ctx, *smalls)
+    )(normed, grads, pre, wide, hid, tall, *smalls)
 
 
 def per_device(
@@ -666,9 +728,10 @@
     hidden = up_weight.shape[1]
     TP, Z = lax.axis_size("tp"), lax.axis_size("seq")
     tokens = R * S * TP * Z
+    inside = attention_inside(R * TP * Z)
     weights = jnp.swapaxes(attend_weight, 0, 1)
     (
-        normed, grads, hid, pre, ctx, dproj, *smalls
+        normed, grads, hid, pre, wide, tall, *smalls
     ) = block_call(
         stream, cotangent, norm_gain.reshape(1, D), norm_offset.reshape(1, D),
         final_bias.reshape(1, D), attend_bias, up_bias.reshape(1, hidden),
@@ -679,8 +742,8 @@
         result, stream_grad, gain_grad, offset_grad, fbias_grad, abias_grad, ubias_grad,
     ) = weight_call(
         normed.reshape(tokens, D), grads.reshape(tokens, D), pre.reshape(tokens, hidden),
-        dproj.reshape(3, tokens, local), hid.reshape(tokens, hidden), ctx.reshape(tokens, local),
-        smalls,
+        wide if inside else wide.reshape(3, tokens, local), hid.reshape(tokens, hidden),
+        tall if inside else tall.reshape(tokens, local), smalls, local, inside,
     )
     return (
         result,

time: 181 us -> 174 us (0.961)
  Pallas kernels: 180 us -> 173 us
    pallas_call x1, Pallas kernels: 36.5 us -> 28.7 us  [weight_call(): pl.pallas_call(functools.partial(weight_kernel, steps, inside), grid=(2 *...]
where the time goes in v5:
time: 174 us
  Pallas kernels  173 us (99%)
    pallas_call x1, Pallas kernels, block_call(): pl.pallas_call(functools.partial(block_kernel, (Z, TP, S, R, D)), in_spec...  144 us
    pallas_call x1, Pallas kernels, weight_call(): pl.pallas_call(functools.partial(weight_kernel, steps, inside), grid=(2 *...  28.7 us

profile of v5, /device:TPU:0, one launch (start us, length us, event | category | flops | bytes accessed | tf_op | source)
XLA Modules:
  0.0 174.0 jit_solution(5428735522306894376)
XLA Ops:
  0.6 144.5 %block.1 = (bf16[4,4,8,16,2048]{4,3,2,1,0:T(8,128)(2,1)}, bf16[4,4,8,16,2048]{4,3,2,1,0:T(8,128)(2,1)}, bf16[4,512,1024]{2,1,0:T(8,128)(2,1)}, bf16[4,512,1024]{...) custom-call(f32[16,4,2048]{2,1,0:T(4,128)} %stream_ref.1, ...), custom_call_target="tpu_custom_call" | custom-call | tf_op jit(solution)/shard_map/block/pallas_call | solution.py:564
  145.2 28.7 %weights.1 = (f32[2048,1024]{1,0:T(8,128)}, f32[3,2048,256]{2,1,0:T(8,128)}, f32[1024,2048]{1,0:T(8,128)}, f32[256,2048]{1,0:T(8,128)}, f32[16,4,2048]{2,1,0:T(4...) custom-call(bf16[2048,2048]{1,0:T(8,128)(2,1)} %bitcast.14, ...), custom_call_target="tpu_custom_call" | custom-call | tf_op jit(solution)/shard_map/weights/pallas_call | solution.py:677

commit v6 on v5

--- a/solution.py
+++ b/solution.py
@@ -302,12 +302,12 @@
     lead = 2 * levels
 
     def run_groups(s, part):
-        for k in range(Z * part // 4, Z * (part + 1) // 4):
-            for i, step in group_steps(Z + lead + k):
-
-                @pl.when(s + i < S)
-                def _(step=step, i=i):
-                    step(s + i)
+        steps = [step for k in range(Z) for step in group_steps(Z + lead + k)]
+        for i, step in steps[len(steps) * part // 8 : len(steps) * (part + 1) // 8]:
+
+            @pl.when(s + i < S)
+            def _(step=step, i=i):
+                step(s + i)
 
     z_sends(0)
     own_unit(0, 0)
@@ -326,6 +326,7 @@
     table[1] = jnp.where(lane < half, -sine, jnp.where(lane < ROT, sine, 0.0))
     abg_ref[...] = jnp.zeros_like(abg_ref)
     ubg[...] = jnp.zeros_like(ubg)
+    sum_tp[t] = jnp.zeros_like(sum_tp[t])
     for load in loads:
         load.wait()
 
@@ -335,140 +336,7 @@
                 step(i)
     end_step(0)
 
-    def turned(x, sign):
-        first = lax.broadcasted_iota(jnp.int32, (1, pair), 1) % HEAD_DIM < half
-        crossed = jnp.where(first, pltpu.roll(x, pair - half, 1), pltpu.roll(x, half, 1))
-        return x * table[0] + sign * (crossed * table[1])
-
-    @pl.loop(0, S)
-    def _(s):
-        kept = s if inside else 0
-
-        def rows_n():
-            return gat[0, s].reshape(L, D)
-
-        def rows_g():
-            return gat[1, s].reshape(L, D)
-
-        @pl.when(s > 0)
-        def _():
-            for copy in out_copies(s - 1):
-                copy.wait()
-
-        @pl.loop(0, 3)
-        def _(j):
-            proj[j] = dot(rows_n(), wa[j], (1, 0)) + abias_ref[pl.ds(j, 1), :]
-
-        cgrad[...] = dot(rows_g(), wo[...], (1, 1)).astype(BF)
-
-        @pl.when(s > 0)
-        def _():
-            p_sends(s - 1)
-
-        @pl.loop(0, local // pair)
-        def _(h):
-            lanes = pl.ds(pl.multiple_of(h * pair, pair), pair)
-            q = turned(proj[0, :, lanes], 1.0).astype(BF)
-            k = turned(proj[1, :, lanes], 1.0).astype(BF)
-            v = proj[2, :, lanes].astype(BF)
-            c, dq, dk, dv = head_pass(q, k, v, cgrad[:, lanes], pair // HEAD_DIM)
-            ctx[kept, :, lanes] = c
-            for j, value in enumerate((turned(dq, -1.0), turned(dk, -1.0), dv)):
-                dproj[j, kept, :, lanes] = value.astype(BF)
-                abg_ref[j : j + 1, lanes] += jnp.sum(value, axis=0, keepdims=True)
-
-            @pl.when(h == 0)
-            def _():
-                run_groups(s, 0)
-
-        tile = 256 if L <= 512 else 128
-        middle = hidden // tile // 2
-
-        def feed_forward(n):
-            cols = pl.ds(pl.multiple_of(n * tile, tile), tile)
-            value, slope = gelu_parts(dot(rows_n(), wu[:, cols], (1, 0)) + ubias_ref[:, cols])
-            hid[:, cols] = value.astype(BF)
-            grad = dot(rows_g(), wd[cols, :], (1, 1)) * slope
-            pre[:, cols] = grad.astype(BF)
-            ubg[:, cols] += jnp.sum(grad, axis=0, keepdims=True)
-
-        @pl.loop(0, hidden // tile)
-        def _(n):
-            feed_forward(n)
-
-            @pl.when(n == 0)
-            def _():
-                run_groups(s, 1)
-
-            @pl.when(n == middle)
-            def _():
-                run_groups(s, 2)
-
-        for copy in out_copies(s):
-            copy.start()
-
-        mine = pl.ds(pl.multiple_of(z * own_rows, own_rows), own_rows)
-
-        @pl.loop(0, D // 256)
-        def _(n):
-            cols = pl.ds(pl.multiple_of(n * 256, 256), 256)
-            out = dot(ctx[kept, mine, :], wo[:, cols], (1, 0)) + dot(hid[mine, :], wd[:, cols], (1, 0))
-            back = dot(pre[mine, :], wu[cols, :], (1, 1))
-            for j in range(3):
-                back = back + dot(dproj[j, kept, mine, :], wa[j, cols, :], (1, 1))
-            part[0, s, :, :, :, cols] = out.astype(BF).reshape(chips, 2, R, 256)
-            part[1, s, :, :, :, cols] = back.astype(BF).reshape(chips, 2, R, 256)
-
-        half_sends(s)
-
-        run_groups(s, 3)
-
-        @pl.when(s + 1 < S)
-        def _():
-            end_step(s + 1)
-
-    strip = D // 4
-
-    def strip_of(n):
-        return pl.ds(pl.multiple_of(n * strip, strip), strip)
-
-    def tall_copy():
-        return pltpu.make_async_copy(tall, tall_out, gs.at[2])
-
-    def wide_copy(n, slot):
-        return pltpu.make_async_copy(wide.at[slot], wide_out.at[:, strip_of(n), :], gs.at[slot])
-
-    def output_grads():
-        if inside:
-
-            @pl.loop(0, 4)
-            def _(n):
-                rows = gat[1, :, :, :, :, strip_of(n)].reshape(S * L, strip)
-                tall[:, strip_of(n)] = dot(ctx[...].reshape(S * L, local), rows, (0, 0))
-
-            tall_copy().start()
-
-    def attend_grads(n, slot):
-        if inside:
-
-            @pl.loop(0, 3)
-            def _(j):
-                rows = gat[0, :, :, :, :, strip_of(n)].reshape(S * L, strip)
-                wide[slot, j] = dot(rows, dproj[j].reshape(S * L, local), (0, 0))
-
-            wide_copy(n, slot).start()
-
-    output_grads()
-    p_sends(S - 1)
-
-    @pl.loop(0, 2)
-    def _(n):
-        attend_grads(n, n)
-
-    sum_tp[t] = jnp.zeros_like(sum_tp[t])
-
-    @pl.loop(0, S)
-    def _(s):
+    def finish_sequence(s):
         totals = []
         for kind in range(2):
             incoming = parts_in.at[kind, s, pl.ds(0, chips - 1)]
@@ -494,6 +362,146 @@
         ).reshape(R, 1, D)
         for i, value in enumerate((ngrad * u, ngrad, cot)):
             sum_tp[t, i] += jnp.sum(value, axis=0, keepdims=True).reshape(D // 128, 128)
+
+    def turned(x, sign):
+        first = lax.broadcasted_iota(jnp.int32, (1, pair), 1) % HEAD_DIM < half
+        crossed = jnp.where(first, pltpu.roll(x, pair - half, 1), pltpu.roll(x, half, 1))
+        return x * table[0] + sign * (crossed * table[1])
+
+    @pl.loop(0, S)
+    def _(s):
+        kept = s if inside else 0
+
+        def rows_n():
+            return gat[0, s].reshape(L, D)
+
+        def rows_g():
+            return gat[1, s].reshape(L, D)
+
+        @pl.when(s > 0)
+        def _():
+            for copy in out_copies(s - 1):
+                copy.wait()
+
+        @pl.loop(0, 3)
+        def _(j):
+            proj[j] = dot(rows_n(), wa[j], (1, 0)) + abias_ref[pl.ds(j, 1), :]
+
+        cgrad[...] = dot(rows_g(), wo[...], (1, 1)).astype(BF)
+
+        @pl.when(s > 0)
+        def _():
+            p_sends(s - 1)
+
+        run_groups(s, 0)
+
+        @pl.loop(0, local // pair)
+        def _(h):
+            lanes = pl.ds(pl.multiple_of(h * pair, pair), pair)
+            q = turned(proj[0, :, lanes], 1.0).astype(BF)
+            k = turned(proj[1, :, lanes], 1.0).astype(BF)
+            v = proj[2, :, lanes].astype(BF)
+            c, dq, dk, dv = head_pass(q, k, v, cgrad[:, lanes], pair // HEAD_DIM)
+            ctx[kept, :, lanes] = c
+            for j, value in enumerate((turned(dq, -1.0), turned(dk, -1.0), dv)):
+                dproj[j, kept, :, lanes] = value.astype(BF)
+                abg_ref[j : j + 1, lanes] += jnp.sum(value, axis=0, keepdims=True)
+
+            @pl.when(h == 0)
+            def _():
+                run_groups(s, 1)
+
+        run_groups(s, 2)
+        tile = min(hidden, 512 if L <= 512 else 128)
+        tiles = hidden // tile
+
+        def feed_forward(n):
+            cols = pl.ds(pl.multiple_of(n * tile, tile), tile)
+            value, slope = gelu_parts(dot(rows_n(), wu[:, cols], (1, 0)) + ubias_ref[:, cols])
+            hid[:, cols] = value.astype(BF)
+            grad = dot(rows_g(), wd[cols, :], (1, 1)) * slope
+            pre[:, cols] = grad.astype(BF)
+            ubg[:, cols] += jnp.sum(grad, axis=0, keepdims=True)
+
+        @pl.loop(0, tiles)
+        def _(n):
+            feed_forward(n)
+
+            for q in range(tiles):
+
+                @pl.when(n == q)
+                def _(q=q):
+                    for part in range(4 * q // tiles, 4 * (q + 1) // tiles):
+                        run_groups(s, 3 + part)
+
+        for copy in out_copies(s):
+            copy.start()
+
+        mine = pl.ds(pl.multiple_of(z * own_rows, own_rows), own_rows)
+
+        @pl.loop(0, D // 256)
+        def _(n):
+            cols = pl.ds(pl.multiple_of(n * 256, 256), 256)
+            out = dot(ctx[kept, mine, :], wo[:, cols], (1, 0)) + dot(hid[mine, :], wd[:, cols], (1, 0))
+            back = dot(pre[mine, :], wu[cols, :], (1, 1))
+            for j in range(3):
+                back = back + dot(dproj[j, kept, mine, :], wa[j, cols, :], (1, 1))
+            part[0, s, :, :, :, cols] = out.astype(BF).reshape(chips, 2, R, 256)
+            part[1, s, :, :, :, cols] = back.astype(BF).reshape(chips, 2, R, 256)
+
+        half_sends(s)
+
+        run_groups(s, 7)
+
+        @pl.when(s >= 2)
+        def _():
+            finish_sequence(s - 2)
+
+        @pl.when(s + 1 < S)
+        def _():
+            end_step(s + 1)
+
+    strip = D // 4
+
+    def strip_of(n):
+        return pl.ds(pl.multiple_of(n * strip, strip), strip)
+
+    def tall_copy():
+        return pltpu.make_async_copy(tall, tall_out, gs.at[2])
+
+    def wide_copy(n, slot):
+        return pltpu.make_async_copy(wide.at[slot], wide_out.at[:, strip_of(n), :], gs.at[slot])
+
+    def output_grads():
+        if inside:
+
+            @pl.loop(0, 4)
+            def _(n):
+                rows = gat[1, :, :, :, :, strip_of(n)].reshape(S * L, strip)
+                tall[:, strip_of(n)] = dot(ctx[...].reshape(S * L, local), rows, (0, 0))
+
+            tall_copy().start()
+
+    def attend_grads(n, slot):
+        if inside:
+
+            @pl.loop(0, 3)
+            def _(j):
+                rows = gat[0, :, :, :, :, strip_of(n)].reshape(S * L, strip)
+                wide[slot, j] = dot(rows, dproj[j].reshape(S * L, local), (0, 0))
+
+            wide_copy(n, slot).start()
+
+    output_grads()
+    p_sends(S - 1)
+
+    @pl.loop(0, 2)
+    def _(n):
+        attend_grads(n, n)
+
+    @pl.loop(max(0, S - 2), S)
+    def _(s):
+        finish_sequence(s)
 
     def m_copy(d):
         return remote(sum_tp.at[t], sum_tp.at[t], ms.at[d], mr.at[0], {"tp": (t + d) % TP})

time: 174 us -> 169 us (0.971)
  Pallas kernels: 173 us -> 168 us
    pallas_call x1, Pallas kernels: 144 us -> 139 us  [block_call(): pl.pallas_call(functools.partial(block_kernel, (Z, TP, S, R, D)), in_spec...]
where the time goes in v6:
time: 169 us
  Pallas kernels  168 us (99%)
    pallas_call x1, Pallas kernels, block_call(): pl.pallas_call(functools.partial(block_kernel, (Z, TP, S, R, D)), in_spec...  139 us
    pallas_call x1, Pallas kernels, weight_call(): pl.pallas_call(functools.partial(weight_kernel, steps, inside), grid=(2 *...  28.7 us

profile of v6, /device:TPU:0, one launch (start us, length us, event | category | flops | bytes accessed | tf_op | source)
XLA Modules:
  0.0 168.7 jit_solution(9280909699865021289)
XLA Ops:
  0.6 139.2 %block.1 = (bf16[4,4,8,16,2048]{4,3,2,1,0:T(8,128)(2,1)}, bf16[4,4,8,16,2048]{4,3,2,1,0:T(8,128)(2,1)}, bf16[4,512,1024]{2,1,0:T(8,128)(2,1)}, bf16[4,512,1024]{...) custom-call(f32[16,4,2048]{2,1,0:T(4,128)} %stream_ref.1, ...), custom_call_target="tpu_custom_call" | custom-call | tf_op jit(solution)/shard_map/block/pallas_call | solution.py:572
  139.9 28.7 %weights.1 = (f32[2048,1024]{1,0:T(8,128)}, f32[3,2048,256]{2,1,0:T(8,128)}, f32[1024,2048]{1,0:T(8,128)}, f32[256,2048]{1,0:T(8,128)}, f32[16,4,2048]{2,1,0:T(4...) custom-call(bf16[2048,2048]{1,0:T(8,128)(2,1)} %bitcast.14, ...), custom_call_target="tpu_custom_call" | custom-call | tf_op jit(solution)/shard_map/weights/pallas_call | solution.py:685

commit v7 on v6

--- a/solution.py
+++ b/solution.py
@@ -143,7 +143,10 @@
 
     loads = [
         pltpu.make_async_copy(src, dst, ws.at[i])
-        for i, (src, dst) in enumerate(((wa_hbm, wa), (wo_hbm, wo), (wu_hbm, wu), (wd_hbm, wd)))
+        for i, (src, dst) in enumerate(((wo_hbm, wo), (wu_hbm, wu), (wd_hbm, wd)))
+    ] + [
+        pltpu.make_async_copy(wa_hbm.at[j], wa.at[:, pl.ds(j * wo.shape[0], wo.shape[0])], ws.at[3 + j])
+        for j in range(3)
     ]
     for load in loads:
         load.start()
@@ -383,9 +386,14 @@
             for copy in out_copies(s - 1):
                 copy.wait()
 
-        @pl.loop(0, 3)
-        def _(j):
-            proj[j] = dot(rows_n(), wa[j], (1, 0)) + abias_ref[pl.ds(j, 1), :]
+        together = 3 if inside else 1
+        for first in range(0, 3, together):
+            wide_proj = dot(rows_n(), wa[:, first * local : (first + together) * local], (1, 0))
+            for j in range(together):
+                proj[first + j] = (
+                    wide_proj[:, j * local : (j + 1) * local]
+                    + abias_ref[first + j : first + j + 1, :]
+                )
 
         cgrad[...] = dot(rows_g(), wo[...], (1, 1)).astype(BF)
 
@@ -439,15 +447,17 @@
 
         mine = pl.ds(pl.multiple_of(z * own_rows, own_rows), own_rows)
 
-        @pl.loop(0, D // 256)
+        step = 512 if inside else 256
+
+        @pl.loop(0, D // step)
         def _(n):
-            cols = pl.ds(pl.multiple_of(n * 256, 256), 256)
+            cols = pl.ds(pl.multiple_of(n * step, step), step)
             out = dot(ctx[kept, mine, :], wo[:, cols], (1, 0)) + dot(hid[mine, :], wd[:, cols], (1, 0))
             back = dot(pre[mine, :], wu[cols, :], (1, 1))
             for j in range(3):
-                back = back + dot(dproj[j, kept, mine, :], wa[j, cols, :], (1, 1))
-            part[0, s, :, :, :, cols] = out.astype(BF).reshape(chips, 2, R, 256)
-            part[1, s, :, :, :, cols] = back.astype(BF).reshape(chips, 2, R, 256)
+                back = back + dot(dproj[j, kept, mine, :], wa[cols, j * local : (j + 1) * local], (1, 1))
+            part[0, s, :, :, :, cols] = out.astype(BF).reshape(chips, 2, R, step)
+            part[1, s, :, :, :, cols] = back.astype(BF).reshape(chips, 2, R, step)
 
         half_sends(s)
 
@@ -590,7 +600,7 @@
         ],
         scratch_shapes=[
             pltpu.VMEM((2, S, Z, TP, R, D), BF),
-            pltpu.VMEM((3, D, local), BF),
+            pltpu.VMEM((D, 3 * local), BF),
             pltpu.VMEM((local, D), BF),
             pltpu.VMEM((D, hidden), BF),
             pltpu.VMEM((hidden, D), BF),
@@ -622,7 +632,7 @@
             dma((2, S)),
             dma((TP + Z,)),
             dma((2,)),
-            dma((4,)),
+            dma((6,)),
             dma((6,)),
             dma((3,)),
         ],

time: 169 us -> 168 us (level)
  Pallas kernels: 168 us -> 166 us
where the time goes in v7:
time: 168 us; the launch traced here: 167 us
  Pallas kernels  166 us (99%)
    pallas_call x1, Pallas kernels, block_call(): pl.pallas_call(functools.partial(block_kernel, (Z, TP, S, R, D)), in_spec...  138 us
    pallas_call x1, Pallas kernels, weight_call(): pl.pallas_call(functools.partial(weight_kernel, steps, inside), grid=(2 *...  28.5 us

profile of v7, /device:TPU:0, one launch (start us, length us, event | category | flops | bytes accessed | tf_op | source)
XLA Modules:
  0.0 167.3 jit_solution(15553882173866703143)
XLA Ops:
  0.6 137.9 %block.1 = (bf16[4,4,8,16,2048]{4,3,2,1,0:T(8,128)(2,1)}, bf16[4,4,8,16,2048]{4,3,2,1,0:T(8,128)(2,1)}, bf16[4,512,1024]{2,1,0:T(8,128)(2,1)}, bf16[4,512,1024]{...) custom-call(f32[16,4,2048]{2,1,0:T(4,128)} %stream_ref.1, ...), custom_call_target="tpu_custom_call" | custom-call | tf_op jit(solution)/shard_map/block/pallas_call | solution.py:582
  138.6 28.5 %weights.1 = (f32[2048,1024]{1,0:T(8,128)}, f32[3,2048,256]{2,1,0:T(8,128)}, f32[1024,2048]{1,0:T(8,128)}, f32[256,2048]{1,0:T(8,128)}, f32[16,4,2048]{2,1,0:T(4...) custom-call(bf16[2048,2048]{1,0:T(8,128)(2,1)} %bitcast.14, ...), custom_call_target="tpu_custom_call" | custom-call | tf_op jit(solution)/shard_map/weights/pallas_call | solution.py:695

commit v8 on v7

--- a/solution.py
+++ b/solution.py
@@ -482,15 +482,13 @@
     def wide_copy(n, slot):
         return pltpu.make_async_copy(wide.at[slot], wide_out.at[:, strip_of(n), :], gs.at[slot])
 
-    def output_grads():
+    def output_grads(first, last):
         if inside:
 
-            @pl.loop(0, 4)
+            @pl.loop(first, last)
             def _(n):
                 rows = gat[1, :, :, :, :, strip_of(n)].reshape(S * L, strip)
                 tall[:, strip_of(n)] = dot(ctx[...].reshape(S * L, local), rows, (0, 0))
-
-            tall_copy().start()
 
     def attend_grads(n, slot):
         if inside:
@@ -502,8 +500,11 @@
 
             wide_copy(n, slot).start()
 
-    output_grads()
+    output_grads(0, 2)
     p_sends(S - 1)
+    output_grads(2, 4)
+    if inside:
+        tall_copy().start()
 
     @pl.loop(0, 2)
     def _(n):

time: 168 us -> 167 us (level)
  no operation moved by 1% of the time
where the time goes in v8:
time: 167 us; the launch traced here: 166 us
  Pallas kernels  165 us (99%)
    pallas_call x1, Pallas kernels, block_call(): pl.pallas_call(functools.partial(block_kernel, (Z, TP, S, R, D)), in_spec...  137 us
    pallas_call x1, Pallas kernels, weight_call(): pl.pallas_call(functools.partial(weight_kernel, steps, inside), grid=(2 *...  28.5 us

profile of v8, /device:TPU:0, one launch (start us, length us, event | category | flops | bytes accessed | tf_op | source)
XLA Modules:
  0.0 166.3 jit_solution(7396035764459584320)
XLA Ops:
  0.6 137.0 %block.1 = (bf16[4,4,8,16,2048]{4,3,2,1,0:T(8,128)(2,1)}, bf16[4,4,8,16,2048]{4,3,2,1,0:T(8,128)(2,1)}, bf16[4,512,1024]{2,1,0:T(8,128)(2,1)}, bf16[4,512,1024]{...) custom-call(f32[16,4,2048]{2,1,0:T(4,128)} %stream_ref.1, ...), custom_call_target="tpu_custom_call" | custom-call | tf_op jit(solution)/shard_map/block/pallas_call | solution.py:583
  137.6 28.5 %weights.1 = (f32[2048,1024]{1,0:T(8,128)}, f32[3,2048,256]{2,1,0:T(8,128)}, f32[1024,2048]{1,0:T(8,128)}, f32[256,2048]{1,0:T(8,128)}, f32[16,4,2048]{2,1,0:T(4...) custom-call(bf16[2048,2048]{1,0:T(8,128)(2,1)} %bitcast.14, ...), custom_call_target="tpu_custom_call" | custom-call | tf_op jit(solution)/shard_map/weights/pallas_call | solution.py:696
